TPU v7x, 8 devices: a whole 2x2x1 slice. The times are simulated.
8 devices in a mesh: batch: 1 (over z), z: 2 (over y), y: 2 (over x), x: 2 (over core).
Axes of the slice: x: 2, y: 2, z: 1, core: 2. Of those that a mesh axis runs over, the one named last changes fastest.
Arguments:
- u_init: float32 [64, 64, 64], P(('batch', 'x'), 'y', 'z')
- source: float32 [64, 64, 64], P(('batch', 'x'), 'y', 'z')
- kappa_cell: float32 [64, 64, 64], P(('batch', 'x'), 'y', 'z')
- stencil_w: float32 [26], replicated
- omega_relax: float32 [32], replicated
Outputs:
- output 1: float32 [64, 64, 64], P(('batch', 'x'), 'y', 'z')
- output 2: float32 [32], P('batch')
All inputs are finite; a program needn't handle non-finite values.
Results may differ from a plain program's by a relative error of at most 0.001.
Values are sent between devices in bfloat16 or wider.
A program may use at most 1 GiB of HBM per device.

v0:
```python
import jax
import jax.numpy as jnp
from jax import lax
from jax.sharding import PartitionSpec as P

FIELD_AXES = ('x', 'y', 'z')


def stencil_offsets():
    return [(off_a, off_b, off_c) for off_a in (-1, 0, 1) for off_b in (-1, 0, 1) for off_c in (-1, 0, 1) if (off_a, off_b, off_c) != (0, 0, 0)]


def neighbour_sum(padded, stencil_w, offsets):
    inner_x = padded.shape[0] - 2
    inner_y = padded.shape[1] - 2
    inner_z = padded.shape[2] - 2
    weighted = 0.0
    for term_idx, (off_a, off_b, off_c) in enumerate(offsets):
        shifted = padded[1 + off_a:1 + off_a + inner_x, 1 + off_b:1 + off_b + inner_y, 1 + off_c:1 + off_c + inner_z]
        weighted = weighted + stencil_w[term_idx] * shifted
    return weighted


def exchange(local_block, halo_depth, axis_sizes):
    for dim_idx, mesh_axis in enumerate(FIELD_AXES):
        axis_len = axis_sizes[dim_idx]
        send_up = [(rank_idx, (rank_idx + 1) % axis_len) for rank_idx in range(axis_len)]
        send_down = [(rank_idx, (rank_idx - 1) % axis_len) for rank_idx in range(axis_len)]
        extent = local_block.shape[dim_idx]
        low_ghost = lax.ppermute(lax.slice_in_dim(local_block, extent - halo_depth, extent, axis=dim_idx), mesh_axis, send_up)
        high_ghost = lax.ppermute(lax.slice_in_dim(local_block, 0, halo_depth, axis=dim_idx), mesh_axis, send_down)
        local_block = jnp.concatenate([low_ghost, local_block, high_ghost], axis=dim_idx)
    return local_block


def solution(mesh):
    axis_sizes = (mesh.shape['x'], mesh.shape['y'], mesh.shape['z'])
    field_spec = P(('batch', 'x'), 'y', 'z')

    def local_sweeps(u_local, f_local, kappa_local, stencil_w, omega_relax):
        offsets = stencil_offsets()
        cell_count = u_local.size * axis_sizes[0] * axis_sizes[1] * axis_sizes[2]
        kappa_pad = exchange(kappa_local, 1, axis_sizes)
        diagonal = 0.5 * (kappa_local * jnp.sum(stencil_w) + neighbour_sum(kappa_pad, stencil_w, offsets))
        field_u = u_local
        norm_list = []
        for step_idx in range(omega_relax.shape[0]):
            u_pad = exchange(field_u, 1, axis_sizes)
            near_u = neighbour_sum(u_pad, stencil_w, offsets)
            near_ku = neighbour_sum(kappa_pad * u_pad, stencil_w, offsets)
            applied = diagonal * field_u - 0.5 * (kappa_local * near_u + near_ku)
            residual = f_local - applied
            total_sq = lax.psum(jnp.sum(residual * residual), ('z', 'y', 'x'))
            norm_list.append(jnp.sqrt(total_sq / cell_count))
            field_u = field_u + omega_relax[step_idx] * residual / diagonal
        return field_u, jnp.stack(norm_list)

    return jax.shard_map(local_sweeps, mesh=mesh, in_specs=(field_spec, field_spec, field_spec, P(), P()), out_specs=(field_spec, P('batch')), check_vma=False)
```

profile of v0, /device:TPU:0, one launch (start us, length us, event | category | flops | bytes accessed | tf_op | source)
XLA Modules:
  0.0 1352.9 jit_solution(14404262322148841924)
XLA Ops:
  36.7 29.6 %multiply_reduce_fusion.31 = (f32[]{:T(128)}, f32[32,32,32]{0,2,1:T(8,128)}, f32[32,32,32]{0,2,1:T(8,128)S(1)}) fusion(f32[32,32,32]{0,2,1:T(8,128)S(1)} %copy.110, f32[34,34,34]{0,2,1:T(8,128)S(1)} %get-tuple-element.103, f32[32,32,32]{0,2,1:T(8,128)S(1)} %copy.85, f32[34,34,33]{0,2,1:T(8,128)S(1)} %get-tuple-element.232, f32[]{:T(128)} %bitcast.26, ...), kind=kLoop, calls=%fused_computation.3739 | loop fusion | flops 5505023 | bytes 10371184 | tf_op jit(solution)/shard_map/reduce_sum | solution.py:53
  123.0 22.8 %multiply_reduce_fusion.29 = (f32[]{:T(128)}, f32[32,32,32]{0,2,1:T(8,128)S(1)}) fusion(f32[32,32,32]{0,2,1:T(8,128)S(1)} %copy.110, f32[34,34,34]{0,2,1:T(8,128)S(1)} %maximum_multiply_fusion.2, f32[32,32,32]{0,2,1:T(8,128)} %copy-done, f32[34,34,33]{0,2,1:T(8,128)S(1)} %get-tuple-element.222, f32[]{:T(128)} %bitcast.26, f32[34,33,32]{0,2,1:T(8,128)S(1)} %copy-done.55, ...), kind=kLoop, calls=%fused_computation.3737 | loop fusion | flops 3670015 | bytes 7217260 | tf_op jit(solution)/shard_map/reduce_sum | solution.py:53
  161.4 22.7 %multiply_reduce_fusion.28 = (f32[]{:T(128)}, f32[32,32,32]{0,2,1:T(8,128)S(1)}) fusion(f32[32,32,32]{0,2,1:T(8,128)S(1)} %copy.110, f32[34,34,34]{0,2,1:T(8,128)S(1)} %maximum_multiply_fusion.3, f32[32,32,32]{0,2,1:T(8,128)} %copy-done, f32[34,34,33]{0,2,1:T(8,128)S(1)} %get-tuple-element.218, f32[]{:T(128)} %bitcast.26, f32[34,33,32]{0,2,1:T(8,128)S(1)} %copy-done.56, ...), kind=kLoop, calls=%fused_computation.3736 | loop fusion | flops 3670015 | bytes 7217260 | tf_op jit(solution)/shard_map/reduce_sum | solution.py:53
  200.7 22.8 %multiply_reduce_fusion.27 = (f32[]{:T(128)}, f32[32,32,32]{0,2,1:T(8,128)S(1)}) fusion(f32[32,32,32]{0,2,1:T(8,128)S(1)} %copy.110, f32[34,34,34]{0,2,1:T(8,128)S(1)} %maximum_multiply_fusion.4, f32[32,32,32]{0,2,1:T(8,128)} %copy-done, f32[34,34,33]{0,2,1:T(8,128)S(1)} %get-tuple-element.214, f32[]{:T(128)} %bitcast.26, f32[34,33,32]{0,2,1:T(8,128)S(1)} %copy-done.57, ...), kind=kLoop, calls=%fused_computation.3735 | loop fusion | flops 3670015 | bytes 7217260 | tf_op jit(solution)/shard_map/reduce_sum | solution.py:53
  278.3 23.1 %multiply_reduce_fusion.25 = (f32[]{:T(128)}, f32[32,32,32]{0,2,1:T(8,128)S(1)}) fusion(f32[32,32,32]{0,2,1:T(8,128)S(1)} %copy.110, f32[34,34,34]{0,2,1:T(8,128)S(1)} %maximum_multiply_fusion.6, f32[32,32,32]{0,2,1:T(8,128)} %copy-done, f32[34,34,33]{0,2,1:T(8,128)S(1)} %get-tuple-element.206, f32[]{:T(128)} %bitcast.26, f32[34,33,32]{0,2,1:T(8,128)S(1)} %copy-done.59, ...), kind=kLoop, calls=%fused_computation.3733 | loop fusion | flops 3670015 | bytes 7217260 | tf_op jit(solution)/shard_map/reduce_sum | solution.py:53
  317.0 22.7 %multiply_reduce_fusion.24 = (f32[]{:T(128)}, f32[32,32,32]{0,2,1:T(8,128)S(1)}) fusion(f32[32,32,32]{0,2,1:T(8,128)S(1)} %copy.110, f32[34,34,34]{0,2,1:T(8,128)S(1)} %maximum_multiply_fusion.7, f32[32,32,32]{0,2,1:T(8,128)} %copy-done, f32[34,34,33]{0,2,1:T(8,128)S(1)} %get-tuple-element.202, f32[]{:T(128)} %bitcast.26, f32[34,33,32]{0,2,1:T(8,128)S(1)} %copy-done.60, ...), kind=kLoop, calls=%fused_computation.3732 | loop fusion | flops 3670015 | bytes 7217260 | tf_op jit(solution)/shard_map/reduce_sum | solution.py:53
  356.3 22.8 %multiply_reduce_fusion.23 = (f32[]{:T(128)}, f32[32,32,32]{0,2,1:T(8,128)S(1)}) fusion(f32[32,32,32]{0,2,1:T(8,128)S(1)} %copy.110, f32[34,34,34]{0,2,1:T(8,128)S(1)} %maximum_multiply_fusion.8, f32[32,32,32]{0,2,1:T(8,128)} %copy-done, f32[34,34,33]{0,2,1:T(8,128)S(1)} %get-tuple-element.198, f32[]{:T(128)} %bitcast.26, f32[34,33,32]{0,2,1:T(8,128)S(1)} %copy-done.61, ...), kind=kLoop, calls=%fused_computation.3731 | loop fusion | flops 3670015 | bytes 7217260 | tf_op jit(solution)/shard_map/reduce_sum | solution.py:53
  434.0 22.9 %multiply_reduce_fusion.21 = (f32[]{:T(128)}, f32[32,32,32]{0,2,1:T(8,128)S(1)}) fusion(f32[32,32,32]{0,2,1:T(8,128)S(1)} %copy.110, f32[34,34,34]{0,2,1:T(8,128)S(1)} %maximum_multiply_fusion.10, f32[32,32,32]{0,2,1:T(8,128)} %copy-done, f32[34,34,33]{0,2,1:T(8,128)S(1)} %get-tuple-element.190, f32[]{:T(128)} %bitcast.26, ...), kind=kLoop, calls=%fused_computation.3729 | loop fusion | flops 3670015 | bytes 7217260 | tf_op jit(solution)/shard_map/reduce_sum | solution.py:53
  552.0 22.7 %multiply_reduce_fusion.18 = (f32[]{:T(128)}, f32[32,32,32]{0,2,1:T(8,128)S(1)}) fusion(f32[32,32,32]{0,2,1:T(8,128)S(1)} %copy.110, f32[34,34,34]{0,2,1:T(8,128)S(1)} %maximum_multiply_fusion.13, f32[32,32,32]{0,2,1:T(8,128)} %copy-done, f32[34,34,33]{0,2,1:T(8,128)S(1)} %get-tuple-element.178, f32[]{:T(128)} %bitcast.26, ...), kind=kLoop, calls=%fused_computation.3726 | loop fusion | flops 3670015 | bytes 7217260 | tf_op jit(solution)/shard_map/reduce_sum | solution.py:53
  592.7 22.8 %multiply_reduce_fusion.17 = (f32[]{:T(128)}, f32[32,32,32]{0,2,1:T(8,128)S(1)}) fusion(f32[32,32,32]{0,2,1:T(8,128)S(1)} %copy.110, f32[34,34,34]{0,2,1:T(8,128)S(1)} %maximum_multiply_fusion.14, f32[32,32,32]{0,2,1:T(8,128)} %copy-done, f32[34,34,33]{0,2,1:T(8,128)S(1)} %get-tuple-element.174, f32[]{:T(128)} %bitcast.26, ...), kind=kLoop, calls=%fused_computation.3725 | loop fusion | flops 3670015 | bytes 7217260 | tf_op jit(solution)/shard_map/reduce_sum | solution.py:53
  673.7 22.9 %multiply_reduce_fusion.15 = (f32[]{:T(128)}, f32[32,32,32]{0,2,1:T(8,128)S(1)}) fusion(f32[32,32,32]{0,2,1:T(8,128)S(1)} %copy.110, f32[34,34,34]{0,2,1:T(8,128)S(1)} %maximum_multiply_fusion.16, f32[32,32,32]{0,2,1:T(8,128)} %copy-done, f32[34,34,33]{0,2,1:T(8,128)S(1)} %get-tuple-element.166, f32[]{:T(128)} %bitcast.26, ...), kind=kLoop, calls=%fused_computation.3723 | loop fusion | flops 3670015 | bytes 7217260 | tf_op jit(solution)/shard_map/reduce_sum | solution.py:53
  714.1 22.7 %multiply_reduce_fusion.14 = (f32[]{:T(128)}, f32[32,32,32]{0,2,1:T(8,128)S(1)}) fusion(f32[32,32,32]{0,2,1:T(8,128)S(1)} %copy.110, f32[34,34,34]{0,2,1:T(8,128)S(1)} %maximum_multiply_fusion.17, f32[32,32,32]{0,2,1:T(8,128)} %copy-done, f32[34,34,33]{0,2,1:T(8,128)S(1)} %get-tuple-element.162, f32[]{:T(128)} %bitcast.26, ...), kind=kLoop, calls=%fused_computation.3722 | loop fusion | flops 3670015 | bytes 7217260 | tf_op jit(solution)/shard_map/reduce_sum | solution.py:53
  754.9 23.1 %multiply_reduce_fusion.13 = (f32[]{:T(128)}, f32[32,32,32]{0,2,1:T(8,128)S(1)}) fusion(f32[32,32,32]{0,2,1:T(8,128)S(1)} %copy.110, f32[34,34,34]{0,2,1:T(8,128)S(1)} %maximum_multiply_fusion.18, f32[32,32,32]{0,2,1:T(8,128)} %copy-done, f32[34,34,33]{0,2,1:T(8,128)S(1)} %get-tuple-element.158, f32[]{:T(128)} %bitcast.26, ...), kind=kLoop, calls=%fused_computation.3721 | loop fusion | flops 3670015 | bytes 7217260 | tf_op jit(solution)/shard_map/reduce_sum | solution.py:53
  795.5 22.7 %multiply_reduce_fusion.12 = (f32[]{:T(128)}, f32[32,32,32]{0,2,1:T(8,128)S(1)}) fusion(f32[32,32,32]{0,2,1:T(8,128)S(1)} %copy.110, f32[34,34,34]{0,2,1:T(8,128)S(1)} %maximum_multiply_fusion.19, f32[32,32,32]{0,2,1:T(8,128)} %copy-done, f32[34,34,33]{0,2,1:T(8,128)S(1)} %get-tuple-element.154, f32[]{:T(128)} %bitcast.26, ...), kind=kLoop, calls=%fused_computation.3720 | loop fusion | flops 3670015 | bytes 7217260 | tf_op jit(solution)/shard_map/reduce_sum | solution.py:53
  836.3 22.8 %multiply_reduce_fusion.11 = (f32[]{:T(128)}, f32[32,32,32]{0,2,1:T(8,128)S(1)}) fusion(f32[32,32,32]{0,2,1:T(8,128)S(1)} %copy.110, f32[34,34,34]{0,2,1:T(8,128)S(1)} %maximum_multiply_fusion.20, f32[32,32,32]{0,2,1:T(8,128)} %copy-done, f32[34,34,33]{0,2,1:T(8,128)S(1)} %get-tuple-element.150, f32[]{:T(128)} %bitcast.26, ...), kind=kLoop, calls=%fused_computation.3719 | loop fusion | flops 3670015 | bytes 7217260 | tf_op jit(solution)/shard_map/reduce_sum | solution.py:53
  917.3 22.9 %multiply_reduce_fusion.9 = (f32[]{:T(128)}, f32[32,32,32]{0,2,1:T(8,128)S(1)}) fusion(f32[32,32,32]{0,2,1:T(8,128)S(1)} %copy.110, f32[34,34,34]{0,2,1:T(8,128)S(1)} %maximum_multiply_fusion.22, f32[32,32,32]{0,2,1:T(8,128)} %copy-done, f32[34,34,33]{0,2,1:T(8,128)S(1)} %get-tuple-element.142, f32[]{:T(128)} %bitcast.26, f32[34,33,32]{0,2,1:T(8,128)S(1)} %copy-done.86, ...), kind=kLoop, calls=%fused_computation.3717 | loop fusion | flops 3670015 | bytes 7217260 | tf_op jit(solution)/shard_map/reduce_sum | solution.py:53
  998.6 23.1 %multiply_reduce_fusion.7 = (f32[]{:T(128)}, f32[32,32,32]{0,2,1:T(8,128)S(1)}) fusion(f32[32,32,32]{0,2,1:T(8,128)S(1)} %copy.110, f32[34,34,34]{0,2,1:T(8,128)S(1)} %maximum_multiply_fusion.24, f32[32,32,32]{0,2,1:T(8,128)} %copy-done, f32[34,34,33]{0,2,1:T(8,128)S(1)} %get-tuple-element.134, f32[]{:T(128)} %bitcast.26, f32[34,33,32]{0,2,1:T(8,128)S(1)} %copy-done.90, ...), kind=kLoop, calls=%fused_computation.3715 | loop fusion | flops 3670015 | bytes 7217260 | tf_op jit(solution)/shard_map/reduce_sum | solution.py:53
  1039.2 22.7 %multiply_reduce_fusion.6 = (f32[]{:T(128)}, f32[32,32,32]{0,2,1:T(8,128)S(1)}) fusion(f32[32,32,32]{0,2,1:T(8,128)S(1)} %copy.110, f32[34,34,34]{0,2,1:T(8,128)S(1)} %maximum_multiply_fusion.25, f32[32,32,32]{0,2,1:T(8,128)} %copy-done, f32[34,34,33]{0,2,1:T(8,128)S(1)} %get-tuple-element.130, f32[]{:T(128)} %bitcast.26, f32[34,33,32]{0,2,1:T(8,128)S(1)} %copy-done.92, ...), kind=kLoop, calls=%fused_computation.3714 | loop fusion | flops 3670015 | bytes 7217260 | tf_op jit(solution)/shard_map/reduce_sum | solution.py:53
  1080.0 22.9 %multiply_reduce_fusion.5 = (f32[]{:T(128)}, f32[32,32,32]{0,2,1:T(8,128)S(1)}) fusion(f32[32,32,32]{0,2,1:T(8,128)S(1)} %copy.110, f32[34,34,34]{0,2,1:T(8,128)S(1)} %maximum_multiply_fusion.26, f32[32,32,32]{0,2,1:T(8,128)} %copy-done, f32[34,34,33]{0,2,1:T(8,128)S(1)} %get-tuple-element.126, f32[]{:T(128)} %bitcast.26, f32[34,33,32]{0,2,1:T(8,128)S(1)} %copy-done.94, ...), kind=kLoop, calls=%fused_computation.3713 | loop fusion | flops 3670015 | bytes 7217260 | tf_op jit(solution)/shard_map/reduce_sum | solution.py:53
  1120.4 22.7 %multiply_reduce_fusion.4 = (f32[]{:T(128)}, f32[32,32,32]{0,2,1:T(8,128)S(1)}) fusion(f32[32,32,32]{0,2,1:T(8,128)S(1)} %copy.110, f32[34,34,34]{0,2,1:T(8,128)S(1)} %maximum_multiply_fusion.27, f32[32,32,32]{0,2,1:T(8,128)} %copy-done, f32[34,34,33]{0,2,1:T(8,128)S(1)} %get-tuple-element.122, f32[]{:T(128)} %bitcast.26, f32[34,33,32]{0,2,1:T(8,128)S(1)} %copy-done.96, ...), kind=kLoop, calls=%fused_computation.3712 | loop fusion | flops 3670015 | bytes 7217260 | tf_op jit(solution)/shard_map/reduce_sum | solution.py:53
  1161.2 22.9 %multiply_reduce_fusion.3 = (f32[]{:T(128)}, f32[32,32,32]{0,2,1:T(8,128)S(1)}) fusion(f32[32,32,32]{0,2,1:T(8,128)S(1)} %copy.110, f32[34,34,34]{0,2,1:T(8,128)S(1)} %maximum_multiply_fusion.28, f32[32,32,32]{0,2,1:T(8,128)} %copy-done, f32[34,34,33]{0,2,1:T(8,128)S(1)} %get-tuple-element.118, f32[]{:T(128)} %bitcast.26, f32[34,33,32]{0,2,1:T(8,128)S(1)} %copy-done.98, ...), kind=kLoop, calls=%fused_computation.3711 | loop fusion | flops 3670015 | bytes 7217260 | tf_op jit(solution)/shard_map/reduce_sum | solution.py:53
  1201.6 22.7 %multiply_reduce_fusion.2 = (f32[]{:T(128)}, f32[32,32,32]{0,2,1:T(8,128)S(1)}) fusion(f32[32,32,32]{0,2,1:T(8,128)S(1)} %copy.110, f32[34,34,34]{0,2,1:T(8,128)S(1)} %maximum_multiply_fusion.29, f32[32,32,32]{0,2,1:T(8,128)} %copy-done, f32[34,34,33]{0,2,1:T(8,128)S(1)} %get-tuple-element.114, f32[]{:T(128)} %bitcast.26, ...), kind=kLoop, calls=%fused_computation.3710 | loop fusion | flops 3670015 | bytes 7217260 | tf_op jit(solution)/shard_map/reduce_sum | solution.py:53
  1243.4 22.9 %multiply_reduce_fusion.1 = (f32[]{:T(128)}, f32[32,32,32]{0,2,1:T(8,128)S(1)}) fusion(f32[32,32,32]{0,2,1:T(8,128)S(1)} %copy.110, f32[34,34,34]{0,2,1:T(8,128)S(1)} %maximum_multiply_fusion.30, f32[32,32,32]{0,2,1:T(8,128)} %copy-done, f32[34,34,33]{0,2,1:T(8,128)S(1)} %get-tuple-element.110, f32[]{:T(128)} %bitcast.26, ...), kind=kLoop, calls=%fused_computation.3709 | loop fusion | flops 3670015 | bytes 7217260 | tf_op jit(solution)/shard_map/reduce_sum | solution.py:53
  1305.1 23.3 %all-reduce = (f32[]{:T(128)}, f32[]{:T(128)}, f32[]{:T(128)}, f32[]{:T(128)}, f32[]{:T(128)}, /*index=5*/f32[]{:T(128)}, f32[]{:T(128)}, f32[]{:T(128)}, f32[]{...) all-reduce(f32[]{:T(128)} %get-tuple-element.100, ...), channel_id=1, replica_groups=mesh['batch'=1,'z'=2,'y'=2,'x'=2] {'z','y','x'}, use_global_device_ids=true, to_apply=%region_2.0 | all-reduce | flops 32 | bytes 256 | tf_op jit(solution)/shard_map/psum | solution.py:53
  (996 shorter events, 772.5 us)
Async XLA Ops:
  2.4 11.2 collective-permute-start
  4.3 9.3 collective-permute-start.1
  6.2 10.6 collective-permute-start.6
  7.7 9.1 collective-permute-start.7
  13.7 6.0 collective-permute-start.2
  17.7 5.2 collective-permute-start.8
  20.8 10.5 collective-permute-start.4
  22.5 8.9 collective-permute-start.5
  24.7 6.8 collective-permute-start.10
  26.3 5.3 collective-permute-start.11
  76.0 5.0 collective-permute-start.16
  543.0 5.0 collective-permute-start.88
  583.8 5.0 collective-permute-start.94
  624.0 5.0 collective-permute-start.100
  664.7 5.0 collective-permute-start.106
  705.1 5.0 collective-permute-start.112
  745.9 5.0 collective-permute-start.118
  786.6 5.0 collective-permute-start.124
  827.3 5.0 collective-permute-start.130
  867.6 5.0 collective-permute-start.136
  908.4 5.0 collective-permute-start.142
  989.6 5.0 collective-permute-start.154
  1030.3 5.0 collective-permute-start.160
  1152.3 5.0 collective-permute-start.178
  (282 other events, 1016.0 us)
where the time goes:
time: 1370 us; the launch traced here: 1350 us
  other arithmetic  951 us (69%)
  waiting for transfers between devices  166 us (12%)
  starting transfers between devices  153 us (11%)
  local copies, waits for them, and re-layouts  34.9 us (3%)
  between operations  25.1 us (2%)
  blocking collectives  23.3 us (2%)
    reduce_sum x32, other arithmetic, local_sweeps(): total_sq = lax.psum(jnp.sum(residual * residual), ('z', 'y', 'x'))  733 us
    concatenate x66, other arithmetic, exchange(): jnp.concatenate([low_ghost, local_block, high_ghost], axis=dim_idx)  129 us
    ppermute x99, waiting for transfers between devices, exchange(): lax.ppermute(lax.slice_in_dim(local_block, extent - halo_depth, extent, a...  98.6 us
    ppermute x99, starting transfers between devices, exchange(): lax.ppermute(lax.slice_in_dim(local_block, 0, halo_depth, axis=dim_idx),...  83.2 us
    ppermute x99, starting transfers between devices, exchange(): lax.ppermute(lax.slice_in_dim(local_block, extent - halo_depth, extent, a...  69.9 us
    ppermute x99, waiting for transfers between devices, exchange(): lax.ppermute(lax.slice_in_dim(local_block, 0, halo_depth, axis=dim_idx),...  67.3 us
    mul x32, other arithmetic, local_sweeps(): near_ku = neighbour_sum(kappa_pad * u_pad, stencil_w, offsets)  49.5 us
    add x32, other arithmetic, local_sweeps(): field_u = field_u + omega_relax[step_idx] * residual / diagonal  27.4 us
  transfers between devices with their start and end apart: 198, of which 148 were waited for; matrix products, arithmetic and copies ran while one was open for 7% of the time, Pallas kernels for 0%

commit v1 on v0

v1 whole, which is shorter than its diff:
```python
import jax
import jax.numpy as jnp
from jax import lax
from jax.experimental import pallas as pl
from jax.experimental.pallas import tpu as pltpu
from jax.sharding import PartitionSpec as P

MESH = pl.DeviceIdType.MESH
F32 = jnp.float32
DEPTH = 8
BLOCKS = 4
SWEEPS = 32
CELLS = 64 * 64 * 64
OFFSETS = [(a, b, c) for a in (-1, 0, 1) for b in (-1, 0, 1) for c in (-1, 0, 1) if (a, b, c) != (0, 0, 0)]
TERM = {o: n for n, o in enumerate(OFFSETS)}


def kernel(u_ref, f_ref, k_ref, w_ref, om_ref, out_ref, rho_ref,
           pack, recv_own, kap, fld, coef, src_own, src_div, inv, diag, halo, sums, part, back, back_recv,
           own_send, own_recv, ring_send, ring_recv, back_send, back_recv_sem, sum_send, sum_recv):
    xc = lax.axis_index('x')
    yc = lax.axis_index('y')
    zc = lax.axis_index('z')
    me = 4 * zc + 2 * yc + xc
    turn = (yc + zc) % 2
    my_l = xc + turn * (3 - 2 * xc)
    my_q = 2 * xc + zc

    def slab_device(slab_y, slab_l):
        t = slab_l // 2
        return {'batch': 0, 'z': (slab_y + t) % 2, 'y': slab_y, 'x': slab_l + t * (3 - 2 * slab_l)}

    def ring_device(step):
        s = (4 * yc + my_l + step + 8) % 8
        return slab_device(s // 4, s % 4)

    def device(i):
        return {'batch': 0, 'z': i // 4, 'y': (i // 2) % 2, 'x': i % 2}

    lane = lax.broadcasted_iota(jnp.int32, (32, 128), 1) % 64
    is_first = lane == 0
    is_last = lane == 63

    barrier = pltpu.get_barrier_semaphore()
    for r in range(1, 8):
        pl.semaphore_signal(barrier, inc=1, device_id=device((me + r) % 8), device_id_type=MESH)

    def pack_array(a, ref):
        def body(i, _):
            rows = [ref[pl.ds(4 * i + m, 32, stride=32), :] for m in range(4)]
            pack[a, i] = jnp.concatenate(rows, axis=1)
            return 0
        lax.fori_loop(0, 8, body, 0)

    def own_copy(a, r):
        dest = (my_l + r) % 4
        return pltpu.make_async_remote_copy(
            src_ref=pack.at[a, pl.ds(2 * dest, 2)], dst_ref=recv_own.at[a, my_q],
            send_sem=own_send.at[a, r - 1], recv_sem=own_recv.at[a, r - 1],
            device_id=slab_device(yc, dest), device_id_type=MESH)

    def send_own(a):
        for r in range(1, 4):
            own_copy(a, r).start()
        recv_own[a, my_q] = pack[a, pl.ds(2 * my_l, 2)]

    def put(dst, plane, v):
        v_next = jnp.where(is_last, pltpu.roll(v, 63, 1), pltpu.roll(v, 127, 1))
        v_prev = jnp.where(is_first, pltpu.roll(v, 65, 1), pltpu.roll(v, 1, 1))
        for ver, val in ((0, v_prev), (1, v), (2, v_next)):
            dst[ver, plane, 8:40, :] = val
            dst[ver, plane, 7:8, :] = pltpu.roll(val[24:32], 64, 1)[7:8]
            dst[ver, plane, 40:41, :] = pltpu.roll(val[0:8], 64, 1)[0:1]

    def wait_own(a):
        for r in range(1, 4):
            own_copy(a, r).wait_recv()

    def unpack_own(a, store):
        def body(yy, _):
            for m in range(4):
                v = jnp.concatenate([recv_own[a, q, yy, :, 32 * m:32 * m + 32] for q in range(4)], axis=1)
                store(4 * yy + m, v)
            return 0
        lax.fori_loop(0, 2, body, 0)

    def ring_copy(e, src, side):
        return pltpu.make_async_remote_copy(
            src_ref=src, dst_ref=halo.at[e, side],
            send_sem=ring_send.at[e, side], recv_sem=ring_recv.at[e, side],
            device_id=ring_device(1 if side == 0 else -1), device_id_type=MESH)

    def u_source():
        return fld.at[0, 1, pl.ds(8, 8), pl.ds(8, 32), :]

    pack_array(0, k_ref)
    pl.semaphore_wait(barrier, 7)
    send_own(0)
    pack_array(1, u_ref)
    send_own(1)
    pack_array(2, f_ref)
    send_own(2)

    kap_src = kap.at[1, pl.ds(8, 8), pl.ds(8, 32), :]
    wait_own(0)
    unpack_own(0, lambda y, v: put(kap, 8 + y, v))
    for side in range(2):
        ring_copy(0, kap_src, side).start()
    wait_own(1)
    unpack_own(1, lambda y, v: put(fld.at[0], 8 + y, v))
    for side in range(2):
        ring_copy(2, u_source(), side).start()
    wait_own(2)

    def store_f(y, v):
        src_own[y] = v
    unpack_own(2, store_f)
    for side in range(2):
        ring_copy(1, src_own, side).start()

    def unpack_halo(e, dst):
        for side in range(2):
            def body(j, _):
                put(dst, 16 * side + j, halo[e, side, j])
                return 0
            lax.fori_loop(0, 8, body, 0)

    for side in range(2):
        ring_copy(0, kap_src, side).wait()
    unpack_halo(0, kap)

    half_w = [0.5 * w_ref[n] for n in range(26)]

    def coef_plane(p, _):
        for g in range(4):
            rows = pl.ds(8 * g, 8)
            center = kap[1, p, 8 + 8 * g:16 + 8 * g, :]
            terms = []
            total = None
            for n, (ox, oy, oz) in enumerate(OFFSETS):
                near = kap[oz + 1, p + oy, 8 + 8 * g + ox:16 + 8 * g + ox, :]
                c = half_w[n] * (center + near)
                terms.append(c)
                total = c if total is None else total + c
            recip = 1.0 / total
            inv[p, rows, :] = recip
            diag[p, rows, :] = total
            for n in range(26):
                coef[n, p, rows, :] = terms[n] * recip
        return 0
    lax.fori_loop(1, 23, coef_plane, 0)

    for side in range(2):
        ring_copy(1, src_own, side).wait()

    def scale_f(j, _):
        src_div[j] = halo[1, 0, j] * inv[j]
        src_div[8 + j] = src_own[j] * inv[8 + j]
        src_div[16 + j] = halo[1, 1, j] * inv[16 + j]
        return 0
    lax.fori_loop(0, 8, scale_f, 0)

    def load9(b, plane):
        return [[fld[b, oz + 1, plane, 8 + ox:40 + ox, :] for oz in (-1, 0, 1)] for ox in (-1, 0, 1)]

    def gather(acc, near, oy, plane):
        for ox in (-1, 0, 1):
            for oz in (-1, 0, 1):
                if (ox, oy, oz) == (0, 0, 0):
                    acc = acc - near[1][1]
                else:
                    acc = acc + coef[TERM[(ox, oy, oz)], plane] * near[ox + 1][oz + 1]
        return acc

    def segment(b, lo, hi, om, norm, carry):
        def body(m, carry):
            acc0, acc1, total = carry
            near = load9(b, m + 1)
            acc0 = gather(acc0, near, 1, m)
            acc1 = gather(acc1, near, 0, m + 1)
            acc2 = gather(src_div[m + 2], near, -1, m + 2)
            put(fld.at[1 - b], m, fld[b, 1, m, 8:40, :] + om * acc0)
            if norm:
                r = acc0 * diag[m]
                total = total + r * r
            return acc1, acc2, total
        return lax.fori_loop(lo, hi, body, carry)

    def block(blk, _):
        e = 2 + blk
        for side in range(2):
            ring_copy(e, u_source(), side).wait()
        unpack_halo(e, fld.at[0])

        def sweep(i, _):
            b = i % 2
            k = DEPTH * blk + i
            om = om_ref[k]
            lo = 1 + i
            near = load9(b, lo - 1)
            acc0 = gather(src_div[lo], near, -1, lo)
            near = load9(b, lo)
            acc0 = gather(acc0, near, 0, lo)
            acc1 = gather(src_div[lo + 1], near, -1, lo + 1)
            carry = (acc0, acc1, jnp.zeros((32, 128), F32))
            carry = segment(b, lo, 8, om, False, carry)
            carry = segment(b, 8, 16, om, True, carry)
            t = carry[2]
            sums[k] = t[0:8] + t[8:16] + t[16:24] + t[24:32]
            segment(b, 16, 23 - i, om, False, carry)
            return 0
        lax.fori_loop(0, DEPTH, sweep, 0)

        @pl.when(blk < BLOCKS - 1)
        def _():
            for side in range(2):
                ring_copy(e + 1, u_source(), side).start()
        return 0
    lax.fori_loop(0, BLOCKS, block, 0)

    def sum_copy(r):
        return pltpu.make_async_remote_copy(
            src_ref=part.at[8], dst_ref=part.at[me], send_sem=sum_send.at[r - 1], recv_sem=sum_recv.at[r - 1],
            device_id=device((me + r) % 8), device_id_type=MESH)

    flat = jnp.sum(sums[...], axis=1)
    flat = jnp.concatenate([flat, jnp.zeros((96, 128), F32)], axis=0)
    mine = jnp.sum(flat.T, axis=0, keepdims=True)
    mine = jnp.broadcast_to(mine, (8, 128))
    part[8] = mine
    part[me] = mine
    for r in range(1, 8):
        sum_copy(r).start()

    def back_copy(r):
        q = (my_q + r) % 4
        return pltpu.make_async_remote_copy(
            src_ref=back.at[q], dst_ref=back_recv.at[my_l], send_sem=back_send.at[r - 1], recv_sem=back_recv_sem.at[r - 1],
            device_id={'batch': 0, 'z': q % 2, 'y': yc, 'x': q // 2}, device_id_type=MESH)

    for yy in range(2):
        planes = [fld[0, 1, 8 + 4 * yy + m, 8:40, :] for m in range(4)]
        for q in range(4):
            back[q, yy] = jnp.concatenate([v[:, 32 * q:32 * q + 32] for v in planes], axis=1)
    for r in range(1, 4):
        back_copy(r).start()
    back_recv[my_l] = back[my_q]
    for r in range(1, 4):
        back_copy(r).wait()

    def unpack_back(i, _):
        v = back_recv[i // 2, i % 2]
        for m in range(4):
            out_ref[pl.ds(4 * i + m, 32, stride=32), :] = v[:, 32 * m:32 * m + 32]
        return 0
    lax.fori_loop(0, 8, unpack_back, 0)

    for r in range(1, 8):
        sum_copy(r).wait()
    total = part[0]
    for i in range(1, 8):
        total = total + part[i]
    rho_ref[...] = jnp.sqrt(total / CELLS)[0:1, 0:32]

    for a in range(3):
        for r in range(1, 4):
            own_copy(a, r).wait_send()


def solution(mesh):
    field_spec = P(('batch', 'x'), 'y', 'z')

    def local(u, f, kappa, w, om):
        vmem = pl.BlockSpec(memory_space=pltpu.VMEM)
        smem = pl.BlockSpec(memory_space=pltpu.SMEM)
        dma = pltpu.SemaphoreType.DMA
        out, rho = pl.pallas_call(
            kernel,
            out_shape=(jax.ShapeDtypeStruct((1024, 32), F32), jax.ShapeDtypeStruct((1, 32), F32)),
            in_specs=[vmem, vmem, vmem, smem, smem],
            out_specs=(vmem, vmem),
            scratch_shapes=[
                pltpu.VMEM((3, 8, 32, 128), F32),
                pltpu.VMEM((3, 4, 2, 32, 128), F32),
                pltpu.VMEM((3, 24, 48, 128), F32),
                pltpu.VMEM((2, 3, 24, 48, 128), F32),
                pltpu.VMEM((26, 26, 32, 128), F32),
                pltpu.VMEM((8, 32, 128), F32),
                pltpu.VMEM((26, 32, 128), F32),
                pltpu.VMEM((24, 32, 128), F32),
                pltpu.VMEM((24, 32, 128), F32),
                pltpu.VMEM((6, 2, 8, 32, 128), F32),
                pltpu.VMEM((32, 8, 128), F32),
                pltpu.VMEM((9, 8, 128), F32),
                pltpu.VMEM((4, 2, 32, 128), F32),
                pltpu.VMEM((4, 2, 32, 128), F32),
                dma((3, 3)), dma((3, 3)), dma((6, 2)), dma((6, 2)), dma((3,)), dma((3,)), dma((7,)), dma((7,)),
            ],
            compiler_params=pltpu.CompilerParams(collective_id=0, has_side_effects=True),
        )(u.reshape(1024, 32), f.reshape(1024, 32), kappa.reshape(1024, 32), w, om)
        return out.reshape(32, 32, 32), rho.reshape(32)

    return jax.shard_map(local, mesh=mesh, in_specs=(field_spec, field_spec, field_spec, P(), P()),
                         out_specs=(field_spec, P('batch')), check_vma=False)
```

time: 1370 us -> 135 us (0.10); the launches traced: 1350 us -> 134 us
  other arithmetic: 951 us -> 0 us
  waiting for transfers between devices: 166 us -> 0 us
  starting transfers between devices: 153 us -> 0 us
  Pallas kernels: 0 us -> 131 us
  local copies, waits for them, and re-layouts: 34.9 us -> 2.38 us
  between operations: 25.1 us -> 0.65 us
  blocking collectives: 23.3 us -> 0 us
    reduce_sum x33 -> x0, other arithmetic: 734 us -> none  [the longest x32 733 us: local_sweeps(): total_sq = lax.psum(jnp.sum(residual * residual), ('z', 'y', 'x'))]
    ppermute x198 -> x0, waiting for transfers between devices: 166 us -> none  [the longest x99 98.6 us: exchange(): lax.ppermute(lax.slice_in_dim(local_block, extent - halo_depth, extent, a...]
    ppermute x198 -> x0, starting transfers between devices: 153 us -> none  [the longest x99 83.2 us: exchange(): lax.ppermute(lax.slice_in_dim(local_block, 0, halo_depth, axis=dim_idx),...]
    pallas_call x0 -> x1, Pallas kernels: none -> 131 us  [local(): pl.pallas_call(kernel, out_shape=(jax.ShapeDtypeStruct((1024, 32), F32),...]
    concatenate x66 -> x0, other arithmetic: 129 us -> none  [exchange(): jnp.concatenate([low_ghost, local_block, high_ghost], axis=dim_idx)]
    mul x32 -> x0, other arithmetic: 49.5 us -> none  [local_sweeps(): near_ku = neighbour_sum(kappa_pad * u_pad, stencil_w, offsets)]
    add x32 -> x0, other arithmetic: 27.4 us -> none  [local_sweeps(): field_u = field_u + omega_relax[step_idx] * residual / diagonal]
    psum x1 -> x0, blocking collectives: 23.3 us -> none  [local_sweeps(): total_sq = lax.psum(jnp.sum(residual * residual), ('z', 'y', 'x'))]
  transfers between devices with their start and end apart: 198 -> 0, of which waited for: 148 -> 0; matrix products, arithmetic and copies ran while one was open for 7% -> 0% of each run, Pallas kernels for 0% -> 0%
where the time goes in v1:
time: 135 us; the launch traced here: 134 us
  Pallas kernels  131 us (97%)
  local copies, waits for them, and re-layouts  2.38 us (2%)
    pallas_call x1, Pallas kernels, local(): pl.pallas_call(kernel, out_shape=(jax.ShapeDtypeStruct((1024, 32), F32),...  131 us

profile of v1, /device:TPU:0, one launch (start us, length us, event | category | flops | bytes accessed | tf_op | source)
XLA Modules:
  0.0 134.4 jit_solution(12821722515197243959)
XLA Ops:
  0.6 131.3 %shard_map.68 = (f32[1024,32]{1,0:T(8,128)}, f32[1,32]{1,0:T(1,128)}) custom-call(f32[1024,32]{1,0:T(8,128)} %bitcast.6, f32[1024,32]{1,0:T(8,128)} %bitcast.7, f32[1024,32]{1,0:T(8,128)} %bitcast.8, f32[26]{0:T(128)} %w_ref.1, f32[32]{0:T(128)} %om_ref.1), custom_call_target="tpu_custom_call" | custom-call | tf_op jit(solution)/shard_map/pallas_call | solution.py:277
  132.0 0.0 copy-start
  132.0 1.9 %copy.9 = f32[32,32,32]{2,1,0:T(8,128)} copy(f32[32,32,32]{2,1,0:T(8,128)} %bitcast.5) | data formatting | bytes 262144
  133.8 0.0 copy-done
  133.9 0.5 copy.10
Async XLA Ops:
  132.0 1.9 %copy-start = (f32[1,32]{1,0:T(1,128)S(1)}, f32[1,32]{1,0:T(1,128)}, u32[]{:S(2)}) copy-start(f32[1,32]{1,0:T(1,128)} %get-tuple-element.5) | copy-start | bytes 388

commit v2 on v1

--- a/solution.py
+++ b/solution.py
@@ -16,7 +16,7 @@
 
 
 def kernel(u_ref, f_ref, k_ref, w_ref, om_ref, out_ref, rho_ref,
-           pack, recv_own, kap, fld, coef, src_own, src_div, inv, diag, halo, sums, part, back, back_recv,
+           pack, recv_own, kap, fld_a, fld_b, coef, src_own, src_div, inv, diag, halo, sums, part, back, back_recv,
            own_send, own_recv, ring_send, ring_recv, back_send, back_recv_sem, sum_send, sum_recv):
     xc = lax.axis_index('x')
     yc = lax.axis_index('y')
@@ -64,13 +64,21 @@
             own_copy(a, r).start()
         recv_own[a, my_q] = pack[a, pl.ds(2 * my_l, 2)]
 
+    def row(ver, first):
+        return slice(40 * ver + first, 40 * ver + first + 32)
+
     def put(dst, plane, v):
-        v_next = jnp.where(is_last, pltpu.roll(v, 63, 1), pltpu.roll(v, 127, 1))
-        v_prev = jnp.where(is_first, pltpu.roll(v, 65, 1), pltpu.roll(v, 1, 1))
-        for ver, val in ((0, v_prev), (1, v), (2, v_next)):
-            dst[ver, plane, 8:40, :] = val
-            dst[ver, plane, 7:8, :] = pltpu.roll(val[24:32], 64, 1)[7:8]
-            dst[ver, plane, 40:41, :] = pltpu.roll(val[0:8], 64, 1)[0:1]
+        r1, r63, r65, r127 = (pltpu.roll(v, s, 1) for s in (1, 63, 65, 127))
+        dst[plane, row(1, 8), :] = v
+        dst[plane, row(0, 8), :] = jnp.where(is_first, r65, r1)
+        dst[plane, row(2, 8), :] = jnp.where(is_last, r63, r127)
+        low, high, first, last = slice(0, 8), slice(24, 32), is_first[0:8], is_last[0:8]
+        for part, src, dest in ((high, 7, 7), (low, 0, 40)):
+            swap = pltpu.roll(v[part], 64, 1)
+            prev = jnp.where(first, r1[part], r65[part])
+            nxt = jnp.where(last, r127[part], r63[part])
+            for ver, val in ((0, prev), (1, swap), (2, nxt)):
+                dst[plane, 40 * ver + dest:40 * ver + dest + 1, :] = val[src:src + 1]
 
     def wait_own(a):
         for r in range(1, 4):
@@ -91,7 +99,7 @@
             device_id=ring_device(1 if side == 0 else -1), device_id_type=MESH)
 
     def u_source():
-        return fld.at[0, 1, pl.ds(8, 8), pl.ds(8, 32), :]
+        return fld_a.at[pl.ds(8, 8), pl.ds(48, 32), :]
 
     pack_array(0, k_ref)
     pl.semaphore_wait(barrier, 7)
@@ -101,13 +109,13 @@
     pack_array(2, f_ref)
     send_own(2)
 
-    kap_src = kap.at[1, pl.ds(8, 8), pl.ds(8, 32), :]
+    kap_src = kap.at[pl.ds(8, 8), pl.ds(48, 32), :]
     wait_own(0)
     unpack_own(0, lambda y, v: put(kap, 8 + y, v))
     for side in range(2):
         ring_copy(0, kap_src, side).start()
     wait_own(1)
-    unpack_own(1, lambda y, v: put(fld.at[0], 8 + y, v))
+    unpack_own(1, lambda y, v: put(fld_a, 8 + y, v))
     for side in range(2):
         ring_copy(2, u_source(), side).start()
     wait_own(2)
@@ -121,9 +129,10 @@
     def unpack_halo(e, dst):
         for side in range(2):
             def body(j, _):
-                put(dst, 16 * side + j, halo[e, side, j])
+                for m in range(4):
+                    put(dst, 16 * side + 4 * j + m, halo[e, side, 4 * j + m])
                 return 0
-            lax.fori_loop(0, 8, body, 0)
+            lax.fori_loop(0, 2, body, 0)
 
     for side in range(2):
         ring_copy(0, kap_src, side).wait()
@@ -134,19 +143,20 @@
     def coef_plane(p, _):
         for g in range(4):
             rows = pl.ds(8 * g, 8)
-            center = kap[1, p, 8 + 8 * g:16 + 8 * g, :]
+            center = kap[p, 48 + 8 * g:56 + 8 * g, :]
             terms = []
             total = None
             for n, (ox, oy, oz) in enumerate(OFFSETS):
-                near = kap[oz + 1, p + oy, 8 + 8 * g + ox:16 + 8 * g + ox, :]
+                first = 40 * (oz + 1) + 8 + 8 * g + ox
+                near = kap[p + oy, first:first + 8, :]
                 c = half_w[n] * (center + near)
                 terms.append(c)
                 total = c if total is None else total + c
             recip = 1.0 / total
             inv[p, rows, :] = recip
-            diag[p, rows, :] = total
+            diag[p, rows, :] = jnp.where(jnp.logical_and(p >= 8, p < 16), total, 0.0)
             for n in range(26):
-                coef[n, p, rows, :] = terms[n] * recip
+                coef[p, g, 8 * n:8 * n + 8, :] = terms[n] * recip
         return 0
     lax.fori_loop(1, 23, coef_plane, 0)
 
@@ -160,8 +170,8 @@
         return 0
     lax.fori_loop(0, 8, scale_f, 0)
 
-    def load9(b, plane):
-        return [[fld[b, oz + 1, plane, 8 + ox:40 + ox, :] for oz in (-1, 0, 1)] for ox in (-1, 0, 1)]
+    def load9(ref, plane):
+        return [[ref[plane, row(oz + 1, 8 + ox), :] for oz in (-1, 0, 1)] for ox in (-1, 0, 1)]
 
     def gather(acc, near, oy, plane):
         for ox in (-1, 0, 1):
@@ -169,47 +179,63 @@
                 if (ox, oy, oz) == (0, 0, 0):
                     acc = acc - near[1][1]
                 else:
-                    acc = acc + coef[TERM[(ox, oy, oz)], plane] * near[ox + 1][oz + 1]
+                    n = TERM[(ox, oy, oz)]
+                    c = jnp.concatenate([coef[plane, g, 8 * n:8 * n + 8, :] for g in range(4)], axis=0)
+                    acc = acc + c * near[ox + 1][oz + 1]
         return acc
 
-    def segment(b, lo, hi, om, norm, carry):
-        def body(m, carry):
-            acc0, acc1, total = carry
-            near = load9(b, m + 1)
-            acc0 = gather(acc0, near, 1, m)
-            acc1 = gather(acc1, near, 0, m + 1)
-            acc2 = gather(src_div[m + 2], near, -1, m + 2)
-            put(fld.at[1 - b], m, fld[b, 1, m, 8:40, :] + om * acc0)
-            if norm:
-                r = acc0 * diag[m]
-                total = total + r * r
-            return acc1, acc2, total
-        return lax.fori_loop(lo, hi, body, carry)
+    def step(src, dst, om, m, carry):
+        acc0, acc1, total = carry
+        near = load9(src, m + 1)
+        acc0 = gather(acc0, near, 1, m)
+        acc1 = gather(acc1, near, 0, m + 1)
+        acc2 = gather(src_div[m + 2], near, -1, m + 2)
+        dst[m, row(1, 8), :] = src[m, row(1, 8), :] + om * acc0
+        r = acc0 * diag[m]
+        r = r * r
+        total = total + ((r[0:8] + r[8:16]) + (r[16:24] + r[24:32]))
+        return acc1, acc2, total
+
+    def finish(dst, m):
+        put(dst, m, dst[m, row(1, 8), :])
+
+    def sweep(src, dst, i, k):
+        om = om_ref[k]
+        lo = 1 + i
+        near = load9(src, lo - 1)
+        acc0 = gather(src_div[lo], near, -1, lo)
+        near = load9(src, lo)
+        acc0 = gather(acc0, near, 0, lo)
+        acc1 = gather(src_div[lo + 1], near, -1, lo + 1)
+        carry = (acc0, acc1, jnp.zeros((8, 128), F32))
+        if i % 2 == 0:
+            carry = step(src, dst, om, lo, carry)
+            carry = step(src, dst, om, lo + 1, carry)
+            lo = lo + 2
+
+        def body(t, carry):
+            m = lo + 4 * t
+            finish(dst, m - 2)
+            finish(dst, m - 1)
+            carry = step(src, dst, om, m, carry)
+            carry = step(src, dst, om, m + 1, carry)
+            finish(dst, m)
+            finish(dst, m + 1)
+            carry = step(src, dst, om, m + 2, carry)
+            return step(src, dst, om, m + 3, carry)
+        carry = lax.fori_loop(0, (23 - i - lo) // 4, body, carry)
+        sums[k] = carry[2]
+        finish(dst, 21 - i)
+        finish(dst, 22 - i)
 
     def block(blk, _):
         e = 2 + blk
         for side in range(2):
             ring_copy(e, u_source(), side).wait()
-        unpack_halo(e, fld.at[0])
-
-        def sweep(i, _):
-            b = i % 2
-            k = DEPTH * blk + i
-            om = om_ref[k]
-            lo = 1 + i
-            near = load9(b, lo - 1)
-            acc0 = gather(src_div[lo], near, -1, lo)
-            near = load9(b, lo)
-            acc0 = gather(acc0, near, 0, lo)
-            acc1 = gather(src_div[lo + 1], near, -1, lo + 1)
-            carry = (acc0, acc1, jnp.zeros((32, 128), F32))
-            carry = segment(b, lo, 8, om, False, carry)
-            carry = segment(b, 8, 16, om, True, carry)
-            t = carry[2]
-            sums[k] = t[0:8] + t[8:16] + t[16:24] + t[24:32]
-            segment(b, 16, 23 - i, om, False, carry)
-            return 0
-        lax.fori_loop(0, DEPTH, sweep, 0)
+        unpack_halo(e, fld_a)
+        for i in range(DEPTH):
+            src, dst = (fld_a, fld_b) if i % 2 == 0 else (fld_b, fld_a)
+            sweep(src, dst, i, DEPTH * blk + i)
 
         @pl.when(blk < BLOCKS - 1)
         def _():
@@ -239,7 +265,7 @@
             device_id={'batch': 0, 'z': q % 2, 'y': yc, 'x': q // 2}, device_id_type=MESH)
 
     for yy in range(2):
-        planes = [fld[0, 1, 8 + 4 * yy + m, 8:40, :] for m in range(4)]
+        planes = [fld_a[8 + 4 * yy + m, row(1, 8), :] for m in range(4)]
         for q in range(4):
             back[q, yy] = jnp.concatenate([v[:, 32 * q:32 * q + 32] for v in planes], axis=1)
     for r in range(1, 4):
@@ -282,9 +308,10 @@
             scratch_shapes=[
                 pltpu.VMEM((3, 8, 32, 128), F32),
                 pltpu.VMEM((3, 4, 2, 32, 128), F32),
-                pltpu.VMEM((3, 24, 48, 128), F32),
-                pltpu.VMEM((2, 3, 24, 48, 128), F32),
-                pltpu.VMEM((26, 26, 32, 128), F32),
+                pltpu.VMEM((24, 128, 128), F32),
+                pltpu.VMEM((24, 128, 128), F32),
+                pltpu.VMEM((24, 128, 128), F32),
+                pltpu.VMEM((26, 4, 208, 128), F32),
                 pltpu.VMEM((8, 32, 128), F32),
                 pltpu.VMEM((26, 32, 128), F32),
                 pltpu.VMEM((24, 32, 128), F32),

time: 135 us -> 69.4 us (0.51)
  Pallas kernels: 131 us -> 66.2 us
    pallas_call x1, Pallas kernels: 131 us -> 66.2 us  [local(): pl.pallas_call(kernel, out_shape=(jax.ShapeDtypeStruct((1024, 32), F32),...]
where the time goes in v2:
time: 69.4 us; the launch traced here: 69.2 us
  Pallas kernels  66.2 us (95%)
  local copies, waits for them, and re-layouts  2.38 us (3%)
    pallas_call x1, Pallas kernels, local(): pl.pallas_call(kernel, out_shape=(jax.ShapeDtypeStruct((1024, 32), F32),...  66.2 us
    unnamed x4, local copies, waits for them, and re-layouts  2.38 us

profile of v2, /device:TPU:0, one launch (start us, length us, event | category | flops | bytes accessed | tf_op | source)
XLA Modules:
  0.0 69.2 jit_solution(11656069481091695486)
XLA Ops:
  0.6 66.2 %shard_map.68 = (f32[1024,32]{1,0:T(8,128)}, f32[1,32]{1,0:T(1,128)}) custom-call(f32[1024,32]{1,0:T(8,128)} %bitcast.6, f32[1024,32]{1,0:T(8,128)} %bitcast.7, f32[1024,32]{1,0:T(8,128)} %bitcast.8, f32[26]{0:T(128)} %w_ref.1, f32[32]{0:T(128)} %om_ref.1), custom_call_target="tpu_custom_call" | custom-call | tf_op jit(solution)/shard_map/pallas_call | solution.py:303
  66.8 0.0 copy-start
  66.8 1.9 %copy.9 = f32[32,32,32]{2,1,0:T(8,128)} copy(f32[32,32,32]{2,1,0:T(8,128)} %bitcast.5) | data formatting | bytes 262144
  68.7 0.0 copy-done
  68.7 0.5 copy.10
Async XLA Ops:
  66.8 1.9 %copy-start = (f32[1,32]{1,0:T(1,128)S(1)}, f32[1,32]{1,0:T(1,128)}, u32[]{:S(2)}) copy-start(f32[1,32]{1,0:T(1,128)} %get-tuple-element.5) | copy-start | bytes 388

commit v3 on v1

v3 whole, which is shorter than its diff:
```python
import jax
import jax.numpy as jnp
from jax import lax
from jax.experimental import pallas as pl
from jax.experimental.pallas import tpu as pltpu
from jax.sharding import PartitionSpec as P

MESH = pl.DeviceIdType.MESH
F32 = jnp.float32
DEPTH = 8
BLOCKS = 4
SWEEPS = 32
CELLS = 64 * 64 * 64
OFFSETS = [(a, b, c) for a in (-1, 0, 1) for b in (-1, 0, 1) for c in (-1, 0, 1) if (a, b, c) != (0, 0, 0)]
TERM = {o: n for n, o in enumerate(OFFSETS)}


def kernel(u_ref, f_ref, k_ref, w_ref, om_ref, out_ref, rho_ref,
           pack, recv_own, kap, fld_a, fld_b, coef, src_own, src_div, inv, diag, stage, halo, sums, psum, back, back_recv,
           own_send, own_recv, ring_send, ring_recv, back_send, back_recv_sem, sum_send, sum_recv):
    xc = lax.axis_index('x')
    yc = lax.axis_index('y')
    zc = lax.axis_index('z')
    me = 4 * zc + 2 * yc + xc
    turn = (yc + zc) % 2
    my_l = xc + turn * (3 - 2 * xc)
    my_q = 2 * xc + zc

    def slab_device(slab_y, slab_l):
        t = slab_l // 2
        return {'batch': 0, 'z': (slab_y + t) % 2, 'y': slab_y, 'x': slab_l + t * (3 - 2 * slab_l)}

    def ring_device(step):
        s = (4 * yc + my_l + step + 8) % 8
        return slab_device(s // 4, s % 4)

    def device(i):
        return {'batch': 0, 'z': i // 4, 'y': (i // 2) % 2, 'x': i % 2}

    lane = lax.broadcasted_iota(jnp.int32, (1, 32, 128), 2) % 64
    is_first = lane == 0
    is_last = lane == 63

    barrier = pltpu.get_barrier_semaphore()
    for r in range(1, 8):
        pl.semaphore_signal(barrier, inc=1, device_id=device((me + r) % 8), device_id_type=MESH)

    def pack_array(a, ref):
        def body(i, _):
            rows = [ref[pl.ds(4 * i + m, 32, stride=32), :] for m in range(4)]
            pack[a, i] = jnp.concatenate(rows, axis=1)
            return 0
        lax.fori_loop(0, 8, body, 0)

    def own_copy(a, r):
        dest = (my_l + r) % 4
        return pltpu.make_async_remote_copy(
            src_ref=pack.at[a, pl.ds(2 * dest, 2)], dst_ref=recv_own.at[a, my_q],
            send_sem=own_send.at[a, r - 1], recv_sem=own_recv.at[a, r - 1],
            device_id=slab_device(yc, dest), device_id_type=MESH)

    def send_own(a):
        for r in range(1, 4):
            own_copy(a, r).start()
        recv_own[a, my_q] = pack[a, pl.ds(2 * my_l, 2)]

    def row(ver, first):
        return slice(40 * ver + first, 40 * ver + first + 32)

    def put(dst, plane, v):
        planes = pl.ds(plane, v.shape[0])
        r1, r63, r65, r127 = (pltpu.roll(v, s, 2) for s in (1, 63, 65, 127))
        dst[planes, row(1, 8), :] = v
        dst[planes, row(0, 8), :] = jnp.where(is_first, r65, r1)
        dst[planes, row(2, 8), :] = jnp.where(is_last, r63, r127)
        first, last = is_first[:, 0:8], is_last[:, 0:8]
        for rows, src, dest in ((slice(24, 32), 7, 7), (slice(0, 8), 0, 40)):
            swap = pltpu.roll(v[:, rows], 64, 2)
            prev = jnp.where(first, r1[:, rows], r65[:, rows])
            nxt = jnp.where(last, r127[:, rows], r63[:, rows])
            for ver, val in ((0, prev), (1, swap), (2, nxt)):
                dst[planes, 40 * ver + dest:40 * ver + dest + 1, :] = val[:, src:src + 1]

    def wait_own(a):
        for r in range(1, 4):
            own_copy(a, r).wait_recv()

    def unpack_own(a, store):
        def body(yy, _):
            for m in range(4):
                v = jnp.concatenate([recv_own[a, q, yy, :, 32 * m:32 * m + 32] for q in range(4)], axis=1)
                store(4 * yy + m, v)
            return 0
        lax.fori_loop(0, 2, body, 0)

    def ring_copy(e, src, dst, side, part):
        first = 4 * (1 - part) if side == 0 else 4 * part
        return pltpu.make_async_remote_copy(
            src_ref=src(first), dst_ref=dst(side, first),
            send_sem=ring_send.at[e, side, part], recv_sem=ring_recv.at[e, side, part],
            device_id=ring_device(1 if side == 0 else -1), device_id_type=MESH)

    def halo_dst(e):
        return lambda side, first: halo.at[e, side, pl.ds(first, 4)]

    def kap_copy(side, part):
        return ring_copy(0, lambda first: kap.at[pl.ds(8 + first, 4), pl.ds(48, 32), :], halo_dst(0), side, part)

    def f_copy(side, part):
        return ring_copy(1, lambda first: src_own.at[pl.ds(8 + first, 4)],
                         lambda side, first: src_own.at[pl.ds(16 * side + first, 4)], side, part)

    def u_copy(e, side, part):
        return ring_copy(e, lambda first: stage.at[pl.ds(first, 4)], halo_dst(e), side, part)

    PARTS = [(side, part) for part in range(2) for side in range(2)]

    def unpack_halo(e, dst, part):
        for side in range(2):
            j = 4 * (1 - part) if side == 0 else 4 * part
            put(dst, 16 * side + j, halo[e, side, j:j + 4])

    pack_array(0, k_ref)
    pl.semaphore_wait(barrier, 7)
    send_own(0)
    pack_array(1, u_ref)
    send_own(1)
    pack_array(2, f_ref)
    send_own(2)

    wait_own(0)
    unpack_own(0, lambda y, v: put(kap, 8 + y, v[None]))
    for side, part in PARTS:
        kap_copy(side, part).start()
    wait_own(1)

    def store_u(y, v):
        stage[y] = v
        put(fld_a, 8 + y, v[None])
    unpack_own(1, store_u)
    for side, part in PARTS:
        u_copy(2, side, part).start()
    wait_own(2)

    def store_f(y, v):
        src_own[8 + y] = v
    unpack_own(2, store_f)
    for side, part in PARTS:
        f_copy(side, part).start()

    half_w = [0.5 * w_ref[n] for n in range(26)]

    def coef_plane(p, _):
        for g in range(4):
            rows = pl.ds(8 * g, 8)
            center = kap[p, 48 + 8 * g:56 + 8 * g, :]
            terms = []
            total = None
            for n, (ox, oy, oz) in enumerate(OFFSETS):
                first = 40 * (oz + 1) + 8 + 8 * g + ox
                near = kap[p + oy, first:first + 8, :]
                c = half_w[n] * (center + near)
                terms.append(c)
                total = c if total is None else total + c
            recip = 1.0 / total
            inv[p, rows, :] = recip
            diag[p, rows, :] = total
            for n in range(26):
                coef[p, 40 * n + 8 * g:40 * n + 8 * g + 8, :] = terms[n] * recip
        return 0
    def scale_f(p, _):
        src_div[p] = src_own[p] * inv[p]
        return 0

    def coef_range(lo, hi):
        lax.fori_loop(lo, hi, coef_plane, 0)

    def scale_range(lo, hi):
        lax.fori_loop(lo, hi, scale_f, 0)

    sums[...] = jnp.zeros_like(sums)
    coef_range(9, 15)
    scale_range(9, 15)

    def strip(level, blk, lo, n):
        src, dst = (fld_a, fld_b) if level % 2 == 1 else (fld_b, fld_a)
        k = DEPTH * blk + level - 1
        acc = src_div[lo:lo + n] - src[lo:lo + n, row(1, 8), :]
        for ox in (-1, 0, 1):
            for oz in (-1, 0, 1):
                near = src[lo - 1:lo + n + 1, row(oz + 1, 8 + ox), :]
                for oy in (-1, 0, 1):
                    if (ox, oy, oz) != (0, 0, 0):
                        t = TERM[(ox, oy, oz)]
                        acc = acc + coef[lo:lo + n, 40 * t:40 * t + 32, :] * near[1 + oy:1 + oy + n]
        new = src[lo:lo + n, row(1, 8), :] + om_ref[k] * acc
        put(dst, lo, new)
        if level == DEPTH:
            stage[lo - 8:lo - 8 + n] = new
        a, b = max(lo, 8), min(lo + n, 16)
        if a < b:
            r = acc[a - lo:b - lo] * diag[a:b]
            r = jnp.sum(r * r, axis=0)
            sums[k] = sums[k] + ((r[0:8] + r[8:16]) + (r[16:24] + r[24:32]))

    def block(blk, _):
        e = 2 + blk
        for level, lo, n in ((1, 9, 3), (1, 12, 3), (2, 10, 2), (2, 12, 2), (3, 11, 2)):
            strip(level, blk, lo, n)

        for part in range(2):
            @pl.when(blk == 0)
            def _():
                for side in range(2):
                    kap_copy(side, part).wait()
                unpack_halo(0, kap, part)
                left, right = (5, 15) if part == 0 else (1, 19)
                coef_range(left, left + 4)
                coef_range(right, right + 4)
                for side in range(2):
                    f_copy(side, part).wait()
                scale_range(left, left + 4)
                scale_range(right, right + 4)
            for side in range(2):
                u_copy(e, side, part).wait()
            unpack_halo(e, fld_a, part)
            if part == 0:
                for level in range(1, 4):
                    strip(level, blk, 4 + level, 4)
                    strip(level, blk, 16 - level, 4)
                for level in range(4, 7):
                    strip(level, blk, 4 + level, 8 - level)
                    strip(level, blk, 12, 8 - level)
                strip(7, blk, 11, 2)
            else:
                for level in range(1, 9):
                    strip(level, blk, level, 4)
                    strip(level, blk, 20 - level, 4)

        @pl.when(blk < BLOCKS - 1)
        def _():
            for side, part in PARTS:
                u_copy(e + 1, side, part).start()
        return 0
    lax.fori_loop(0, BLOCKS, block, 0)

    def sum_copy(r):
        return pltpu.make_async_remote_copy(
            src_ref=psum.at[8], dst_ref=psum.at[me], send_sem=sum_send.at[r - 1], recv_sem=sum_recv.at[r - 1],
            device_id=device((me + r) % 8), device_id_type=MESH)

    flat = jnp.sum(sums[...], axis=1)
    flat = jnp.concatenate([flat, jnp.zeros((96, 128), F32)], axis=0)
    mine = jnp.sum(flat.T, axis=0, keepdims=True)
    mine = jnp.broadcast_to(mine, (8, 128))
    psum[8] = mine
    psum[me] = mine
    for r in range(1, 8):
        sum_copy(r).start()

    def back_copy(r):
        q = (my_q + r) % 4
        return pltpu.make_async_remote_copy(
            src_ref=back.at[q], dst_ref=back_recv.at[my_l], send_sem=back_send.at[r - 1], recv_sem=back_recv_sem.at[r - 1],
            device_id={'batch': 0, 'z': q % 2, 'y': yc, 'x': q // 2}, device_id_type=MESH)

    for yy in range(2):
        planes = [fld_a[8 + 4 * yy + m, row(1, 8), :] for m in range(4)]
        for q in range(4):
            back[q, yy] = jnp.concatenate([v[:, 32 * q:32 * q + 32] for v in planes], axis=1)
    for r in range(1, 4):
        back_copy(r).start()
    back_recv[my_l] = back[my_q]
    for r in range(1, 4):
        back_copy(r).wait()

    def unpack_back(i, _):
        v = back_recv[i // 2, i % 2]
        for m in range(4):
            out_ref[pl.ds(4 * i + m, 32, stride=32), :] = v[:, 32 * m:32 * m + 32]
        return 0
    lax.fori_loop(0, 8, unpack_back, 0)

    for r in range(1, 8):
        sum_copy(r).wait()
    total = psum[0]
    for i in range(1, 8):
        total = total + psum[i]
    rho_ref[...] = jnp.sqrt(total / CELLS)[0:1, 0:32]

    for a in range(3):
        for r in range(1, 4):
            own_copy(a, r).wait_send()


def solution(mesh):
    field_spec = P(('batch', 'x'), 'y', 'z')

    def local(u, f, kappa, w, om):
        vmem = pl.BlockSpec(memory_space=pltpu.VMEM)
        smem = pl.BlockSpec(memory_space=pltpu.SMEM)
        dma = pltpu.SemaphoreType.DMA
        out, rho = pl.pallas_call(
            kernel,
            out_shape=(jax.ShapeDtypeStruct((1024, 32), F32), jax.ShapeDtypeStruct((1, 32), F32)),
            in_specs=[vmem, vmem, vmem, smem, smem],
            out_specs=(vmem, vmem),
            scratch_shapes=[
                pltpu.VMEM((3, 8, 32, 128), F32),
                pltpu.VMEM((3, 4, 2, 32, 128), F32),
                pltpu.VMEM((24, 128, 128), F32),
                pltpu.VMEM((24, 128, 128), F32),
                pltpu.VMEM((24, 128, 128), F32),
                pltpu.VMEM((24, 1056, 128), F32),
                pltpu.VMEM((24, 32, 128), F32),
                pltpu.VMEM((24, 32, 128), F32),
                pltpu.VMEM((24, 32, 128), F32),
                pltpu.VMEM((24, 32, 128), F32),
                pltpu.VMEM((8, 32, 128), F32),
                pltpu.VMEM((6, 2, 8, 32, 128), F32),
                pltpu.VMEM((32, 8, 128), F32),
                pltpu.VMEM((9, 8, 128), F32),
                pltpu.VMEM((4, 2, 32, 128), F32),
                pltpu.VMEM((4, 2, 32, 128), F32),
                dma((3, 3)), dma((3, 3)), dma((6, 2, 2)), dma((6, 2, 2)), dma((3,)), dma((3,)), dma((7,)), dma((7,)),
            ],
            compiler_params=pltpu.CompilerParams(collective_id=0, has_side_effects=True),
        )(u.reshape(1024, 32), f.reshape(1024, 32), kappa.reshape(1024, 32), w, om)
        return out.reshape(32, 32, 32), rho.reshape(32)

    return jax.shard_map(local, mesh=mesh, in_specs=(field_spec, field_spec, field_spec, P(), P()),
                         out_specs=(field_spec, P('batch')), check_vma=False)
```

time: 135 us -> 57.6 us (0.43)
  Pallas kernels: 131 us -> 54.5 us
    pallas_call x1, Pallas kernels: 131 us -> 54.5 us  [local(): pl.pallas_call(kernel, out_shape=(jax.ShapeDtypeStruct((1024, 32), F32),...]
where the time goes in v3:
time: 57.6 us; the launch traced here: 57.5 us
  Pallas kernels  54.5 us (95%)
  local copies, waits for them, and re-layouts  2.38 us (4%)
  between operations  0.65 us (1%)
    pallas_call x1, Pallas kernels, local(): pl.pallas_call(kernel, out_shape=(jax.ShapeDtypeStruct((1024, 32), F32),...  54.5 us
    unnamed x4, local copies, waits for them, and re-layouts  2.38 us

profile of v3, /device:TPU:0, one launch (start us, length us, event | category | flops | bytes accessed | tf_op | source)
XLA Modules:
  0.0 57.5 jit_solution(5898816919881043114)
XLA Ops:
  0.6 54.5 %shard_map.68 = (f32[1024,32]{1,0:T(8,128)}, f32[1,32]{1,0:T(1,128)}) custom-call(f32[1024,32]{1,0:T(8,128)} %bitcast.6, f32[1024,32]{1,0:T(8,128)} %bitcast.7, f32[1024,32]{1,0:T(8,128)} %bitcast.8, f32[26]{0:T(128)} %w_ref.1, f32[32]{0:T(128)} %om_ref.1), custom_call_target="tpu_custom_call" | custom-call | tf_op jit(solution)/shard_map/pallas_call | solution.py:303
  55.1 0.0 copy-start
  55.1 1.9 %copy.9 = f32[32,32,32]{2,1,0:T(8,128)} copy(f32[32,32,32]{2,1,0:T(8,128)} %bitcast.5) | data formatting | bytes 262144
  57.0 0.0 copy-done
  57.0 0.5 copy.10
Async XLA Ops:
  55.1 1.9 %copy-start = (f32[1,32]{1,0:T(1,128)S(1)}, f32[1,32]{1,0:T(1,128)}, u32[]{:S(2)}) copy-start(f32[1,32]{1,0:T(1,128)} %get-tuple-element.5) | copy-start | bytes 388

commit v4 on v3

v4 whole, which is shorter than its diff:
```python
import jax
import jax.numpy as jnp
from jax import lax
from jax.experimental import pallas as pl
from jax.experimental.pallas import tpu as pltpu
from jax.sharding import PartitionSpec as P

MESH = pl.DeviceIdType.MESH
F32 = jnp.float32
ROWS = 32
LANES = 128
BRICK = 1024
DEPTH = 8
BLOCKS = 4
CELLS = 64 * 64 * 64
OFFSETS = [(a, b, c) for a in (-1, 0, 1) for b in (-1, 0, 1) for c in (-1, 0, 1) if (a, b, c) != (0, 0, 0)]
TERM = {o: n for n, o in enumerate(OFFSETS)}


def kernel(u_ref, f_ref, k_ref, w_hbm, om_hbm, out_ref, rho_ref,
           w_ref, om_ref, bricks, brick_sem, pack, recv_own, kap, fld, coef, src_own, src_div, inv, diag, stage, halo, sums, psum, back, back_recv,
           own_send, own_recv, ring_send, ring_recv, back_send, back_recv_sem, sum_send, sum_recv):
    xc = lax.axis_index('x')
    yc = lax.axis_index('y')
    zc = lax.axis_index('z')
    me = 4 * zc + 2 * yc + xc
    turn = (yc + zc) % 2
    my_l = xc + turn * (3 - 2 * xc)
    my_q = 2 * xc + zc

    def slab_device(slab_y, slab_l):
        t = slab_l // 2
        return {'batch': 0, 'z': (slab_y + t) % 2, 'y': slab_y, 'x': slab_l + t * (3 - 2 * slab_l)}

    def ring_device(step):
        s = (4 * yc + my_l + step + 8) % 8
        return slab_device(s // 4, s % 4)

    def device(i):
        return {'batch': 0, 'z': i // 4, 'y': (i // 2) % 2, 'x': i % 2}

    even = lax.broadcasted_iota(jnp.int32, (1, 8, LANES), 2) % 2 == 0
    top = lax.broadcasted_iota(jnp.int32, (1, 8, LANES), 1) == 0
    lane_in = lax.broadcasted_iota(jnp.int32, (LANES, LANES), 0)
    lane_out = lax.broadcasted_iota(jnp.int32, (LANES, LANES), 1)
    weave = (lane_out == 2 * (lane_in % 64) + lane_in // 64).astype(F32)
    unweave = (lane_in == 2 * (lane_out % 64) + lane_out // 64).astype(F32)

    def move_lanes(v, matrix):
        return jnp.dot(v, matrix, precision=lax.Precision.HIGHEST, preferred_element_type=F32)

    barrier = pltpu.get_barrier_semaphore()
    for r in range(1, 8):
        pl.semaphore_signal(barrier, inc=1, device_id=device((me + r) % 8), device_id_type=MESH)

    loads = [pltpu.make_async_copy(ref, bricks.at[a], brick_sem.at[a]) for a, ref in enumerate((k_ref, u_ref, f_ref))]
    loads.append(pltpu.make_async_copy(w_hbm, w_ref, brick_sem.at[3]))
    loads.append(pltpu.make_async_copy(om_hbm, om_ref, brick_sem.at[4]))
    for load in loads:
        load.start()

    def pack_array(a):
        loads[a].wait()
        for i in range(8):
            rows = [bricks[a, pl.ds(4 * i + m, ROWS, stride=ROWS), :] for m in range(4)]
            pack[a, i] = jnp.concatenate(rows, axis=1)

    def own_copy(a, r):
        dest = (my_l + r) % 4
        return pltpu.make_async_remote_copy(
            src_ref=pack.at[a, pl.ds(2 * dest, 2)], dst_ref=recv_own.at[a, my_q],
            send_sem=own_send.at[a, r - 1], recv_sem=own_recv.at[a, r - 1],
            device_id=slab_device(yc, dest), device_id_type=MESH)

    def send_own(a):
        for r in range(1, 4):
            own_copy(a, r).start()
        recv_own[a, my_q] = pack[a, pl.ds(2 * my_l, 2)]

    def row(ver, first):
        return slice(40 * ver + first, 40 * ver + first + ROWS)

    def put(dst, plane, v):
        dst[pl.ds(plane, v.shape[0]), row(1, 8), :] = v
        put_turned(dst, plane, v)

    def put_turned(dst, plane, v):
        planes = pl.ds(plane, v.shape[0])
        dst[planes, row(0, 8), :] = pltpu.roll(v, 2, 2)
        dst[planes, row(2, 8), :] = pltpu.roll(v, 126, 2)
        edge = jnp.where(top, v[:, 0:8], v[:, 24:ROWS])
        r1, r3, r125, r127 = (pltpu.roll(edge, s, 2) for s in (1, 3, 125, 127))
        for ver, a, b in ((0, r1, r3), (1, r127, r1), (2, r125, r127)):
            swap = jnp.where(even, a, b)
            dst[planes, 40 * ver + 7:40 * ver + 8, :] = swap[:, 7:8]
            dst[planes, 40 * ver + 40:40 * ver + 41, :] = swap[:, 0:1]

    def wait_own(a):
        for r in range(1, 4):
            own_copy(a, r).wait_recv()

    def unpack_own(a, store):
        for yy in range(2):
            for m in range(4):
                v = jnp.concatenate([recv_own[a, q, yy, :, ROWS * m:ROWS * m + ROWS] for q in range(4)], axis=1)
                store(4 * yy + m, move_lanes(v, weave))

    def ring_copy(e, src, dst, side, part):
        first = 4 * (1 - part) if side == 0 else 4 * part
        return pltpu.make_async_remote_copy(
            src_ref=src(first), dst_ref=dst(side, first),
            send_sem=ring_send.at[e, side, part], recv_sem=ring_recv.at[e, side, part],
            device_id=ring_device(1 if side == 0 else -1), device_id_type=MESH)

    def halo_dst(e):
        return lambda side, first: halo.at[e, side, pl.ds(first, 4)]

    def kap_copy(side, part):
        return ring_copy(0, lambda first: kap.at[pl.ds(8 + first, 4), pl.ds(48, ROWS), :], halo_dst(0), side, part)

    def f_copy(side, part):
        return ring_copy(1, lambda first: src_own.at[pl.ds(8 + first, 4)],
                         lambda side, first: src_own.at[pl.ds(16 * side + first, 4)], side, part)

    def u_copy(e, side, part):
        return ring_copy(e, lambda first: stage.at[pl.ds(first, 4)], halo_dst(e), side, part)

    PARTS = [(side, part) for part in range(2) for side in range(2)]

    def unpack_halo(e, dst, part):
        for side in range(2):
            j = 4 * (1 - part) if side == 0 else 4 * part
            put(dst, 16 * side + j, halo[e, side, j:j + 4])

    pack_array(0)
    pl.semaphore_wait(barrier, 7)
    send_own(0)
    pack_array(1)
    send_own(1)
    pack_array(2)
    send_own(2)

    wait_own(0)
    unpack_own(0, lambda y, v: put(kap, 8 + y, v[None]))
    for side in range(2):
        kap_copy(side, 0).start()
    wait_own(1)

    def store_u(y, v):
        stage[y] = v
        put(fld, 8 + y, v[None])
    unpack_own(1, store_u)
    for side in range(2):
        u_copy(2, side, 0).start()
    for side in range(2):
        kap_copy(side, 1).start()
    wait_own(2)

    def store_f(y, v):
        src_own[8 + y] = v
    unpack_own(2, store_f)
    for side in range(2):
        f_copy(side, 0).start()
    for side in range(2):
        u_copy(2, side, 1).start()
    for side in range(2):
        f_copy(side, 1).start()

    loads[3].wait()
    loads[4].wait()
    half_w = [0.5 * w_ref[n] for n in range(26)]

    def coef_plane(p, _):
        for g in range(4):
            rows = pl.ds(8 * g, 8)
            center = kap[p, 48 + 8 * g:56 + 8 * g, :]
            terms = []
            total = None
            for n, (ox, oy, oz) in enumerate(OFFSETS):
                first = 40 * (oz + 1) + 8 + 8 * g + ox
                near = kap[p + oy, first:first + 8, :]
                c = half_w[n] * (center + near)
                terms.append(c)
                total = c if total is None else total + c
            recip = 1.0 / total
            inv[p, rows, :] = recip
            diag[p, rows, :] = jnp.where(jnp.logical_and(p >= 8, p < 16), total, 0.0)
            for n in range(26):
                coef[p, 40 * n + 8 * g:40 * n + 8 * g + 8, :] = terms[n] * recip
        return 0
    def scale_f(p, _):
        src_div[p] = src_own[p] * inv[p]
        return 0

    def coef_range(lo, hi):
        lax.fori_loop(lo, hi, coef_plane, 0)

    def scale_range(lo, hi):
        lax.fori_loop(lo, hi, scale_f, 0)

    sums[...] = jnp.zeros_like(sums)
    coef_range(9, 15)
    scale_range(9, 15)
    for part in range(2):
        for side in range(2):
            kap_copy(side, part).wait()
        unpack_halo(0, kap, part)
        coef_range(*((5, 9) if part == 0 else (1, 5)))
        coef_range(*((15, 19) if part == 0 else (19, 23)))

    def pair(level, first, second, n, before, blk):
        src, dst = (0, 24) if level % 2 == 1 else (24, 0)
        k = DEPTH * blk + level - 1
        om = om_ref[k]
        owned = first + n > 8

        def body(s, _):
            lo = first + s * (second - first)
            last = before + s * (dst + first - before)
            turned = fld[pl.ds(last, 4), row(1, 8), :]
            center = fld[pl.ds(src + lo, n), row(1, 8), :]
            acc = src_div[pl.ds(lo, n)] - center
            for ox in (-1, 0, 1):
                for oz in (-1, 0, 1):
                    near = fld[pl.ds(src + lo - 1, n + 2), row(oz + 1, 8 + ox), :]
                    for oy in (-1, 0, 1):
                        if (ox, oy, oz) != (0, 0, 0):
                            t = 40 * TERM[(ox, oy, oz)]
                            acc = acc + coef[pl.ds(lo, n), t:t + ROWS, :] * near[1 + oy:1 + oy + n]
            new = center + om * acc
            fld[pl.ds(dst + lo, n), row(1, 8), :] = new
            put_turned(fld, last, turned)
            if level == DEPTH:
                stage[pl.ds(lo - 8, n)] = new
            if owned:
                r = acc * diag[pl.ds(lo, n)]
                r = jnp.sum(r * r, axis=0)
                sums[k] = sums[k] + ((r[0:8] + r[8:16]) + (r[16:24] + r[24:ROWS]))
            return 0
        if first == second:
            body(0, 0)
        else:
            lax.fori_loop(0, 2, body, 0)
        return dst + second

    def flush(before):
        put_turned(fld, before, fld[pl.ds(before, 4), row(1, 8), :])
        return before

    def block(blk, _):
        e = 2 + blk
        before = 8
        for level, first, second, n in ((1, 9, 12, 3), (2, 10, 10, 4), (3, 11, 11, 2)):
            before = flush(pair(level, first, second, n, before, blk))
        for part in range(2):
            @pl.when(blk == 0)
            def _():
                left, right = (5, 15) if part == 0 else (1, 19)
                for side in range(2):
                    f_copy(side, part).wait()
                scale_range(left, left + 4)
                scale_range(right, right + 4)
            for side in range(2):
                u_copy(e, side, part).wait()
            unpack_halo(e, fld, part)
            if part == 0:
                for level in range(1, 4):
                    before = pair(level, 4 + level, 16 - level, 4, before, blk)
            else:
                for level in range(1, 9):
                    before = pair(level, level, 20 - level, 4, before, blk)
                    if level < 5:
                        first, second, n = ((8, 12, 4), (9, 12, 3), (10, 10, 4), (11, 11, 2))[level - 1]
                        before = pair(3 + level, first, second, n, before, blk)

        @pl.when(blk < BLOCKS - 1)
        def _():
            for side, part in PARTS:
                u_copy(e + 1, side, part).start()
            flush(before)
        return 0
    lax.fori_loop(0, BLOCKS, block, 0)

    def sum_copy(r):
        return pltpu.make_async_remote_copy(
            src_ref=psum.at[8], dst_ref=psum.at[me], send_sem=sum_send.at[r - 1], recv_sem=sum_recv.at[r - 1],
            device_id=device((me + r) % 8), device_id_type=MESH)

    def back_copy(r):
        q = (my_q + r) % 4
        return pltpu.make_async_remote_copy(
            src_ref=back.at[q], dst_ref=back_recv.at[my_l], send_sem=back_send.at[r - 1], recv_sem=back_recv_sem.at[r - 1],
            device_id={'batch': 0, 'z': q % 2, 'y': yc, 'x': q // 2}, device_id_type=MESH)

    for yy in range(2):
        planes = [move_lanes(fld[8 + 4 * yy + m, row(1, 8), :], unweave) for m in range(4)]
        for q in range(4):
            back[q, yy] = jnp.concatenate([v[:, ROWS * q:ROWS * q + ROWS] for v in planes], axis=1)
    for r in range(1, 4):
        back_copy(r).start()
    back_recv[my_l] = back[my_q]
    flat = jnp.sum(sums[...], axis=1)
    flat = jnp.concatenate([flat, jnp.zeros((96, LANES), F32)], axis=0)
    mine = jnp.sum(flat.T, axis=0, keepdims=True)
    mine = jnp.broadcast_to(mine, (8, LANES))
    psum[8] = mine
    psum[me] = mine
    for r in range(1, 8):
        sum_copy(r).start()

    for r in range(1, 4):
        back_copy(r).wait()
    out_ref[...] = back_recv[...]
    for r in range(1, 8):
        sum_copy(r).wait()
    total = psum[0]
    for i in range(1, 8):
        total = total + psum[i]
    rho_ref[...] = total

    for a in range(3):
        for r in range(1, 4):
            own_copy(a, r).wait_send()


def unpack_kernel(dense_ref, total_ref, out_ref, rho_ref):
    for i in range(8):
        v = dense_ref[i // 2, i % 2]
        for m in range(4):
            out_ref[pl.ds(4 * i + m, ROWS, stride=ROWS), :] = v[:, ROWS * m:ROWS * m + ROWS]
    rho_ref[...] = jnp.sqrt(total_ref[...] / CELLS)[0:1, 0:ROWS]


def solution(mesh):
    field_spec = P(('batch', 'x'), 'y', 'z')

    def local(u, f, kappa, w, om):
        vmem = pl.BlockSpec(memory_space=pltpu.VMEM)
        hbm = pl.BlockSpec(memory_space=pltpu.HBM)
        dma = pltpu.SemaphoreType.DMA
        dense, total = pl.pallas_call(
            kernel,
            out_shape=(pltpu.VMEM((4, 2, ROWS, LANES), F32), pltpu.VMEM((8, LANES), F32)),
            in_specs=[hbm] * 5,
            out_specs=(vmem, vmem),
            scratch_shapes=[
                pltpu.SMEM((26,), F32),
                pltpu.SMEM((ROWS,), F32),
                pltpu.VMEM((3, BRICK, ROWS), F32),
                dma((5,)),
                pltpu.VMEM((3, 8, ROWS, LANES), F32),
                pltpu.VMEM((3, 4, 2, ROWS, LANES), F32),
                pltpu.VMEM((24, LANES, LANES), F32),
                pltpu.VMEM((48, LANES, LANES), F32),
                pltpu.VMEM((24, 1056, LANES), F32),
                pltpu.VMEM((24, ROWS, LANES), F32),
                pltpu.VMEM((24, ROWS, LANES), F32),
                pltpu.VMEM((24, ROWS, LANES), F32),
                pltpu.VMEM((24, ROWS, LANES), F32),
                pltpu.VMEM((8, ROWS, LANES), F32),
                pltpu.VMEM((6, 2, 8, ROWS, LANES), F32),
                pltpu.VMEM((ROWS, 8, LANES), F32),
                pltpu.VMEM((9, 8, LANES), F32),
                pltpu.VMEM((4, 2, ROWS, LANES), F32),
                pltpu.VMEM((4, 2, ROWS, LANES), F32),
                dma((3, 3)), dma((3, 3)), dma((6, 2, 2)), dma((6, 2, 2)), dma((3,)), dma((3,)), dma((7,)), dma((7,)),
            ],
            compiler_params=pltpu.CompilerParams(collective_id=0, has_side_effects=True, vmem_limit_bytes=60 * BRICK * BRICK),
        )(u.reshape(BRICK, ROWS), f.reshape(BRICK, ROWS), kappa.reshape(BRICK, ROWS), w, om)
        out, rho = pl.pallas_call(
            unpack_kernel,
            out_shape=(jax.ShapeDtypeStruct((BRICK, ROWS), F32), jax.ShapeDtypeStruct((1, ROWS), F32)),
            in_specs=[vmem, vmem],
            out_specs=(vmem, vmem),
            compiler_params=pltpu.CompilerParams(vmem_limit_bytes=8 * BRICK * BRICK),
        )(dense, total)
        return out.reshape(ROWS, ROWS, ROWS), rho.reshape(ROWS)

    return jax.shard_map(local, mesh=mesh, in_specs=(field_spec, field_spec, field_spec, P(), P()),
                         out_specs=(field_spec, P('batch')), check_vma=False)
```

time: 57.6 us -> 51.1 us (0.89)
  Pallas kernels: 54.5 us -> 50.3 us
  local copies, waits for them, and re-layouts: 2.38 us -> 0 us
    pallas_call x1 -> x2, Pallas kernels: 54.5 us -> 50.3 us  [the longest x1 49 us: local(): pl.pallas_call(kernel, out_shape=(pltpu.VMEM((4, 2, ROWS, LANES), F32), p...]
    unnamed x4 -> x0, local copies, waits for them, and re-layouts: 2.38 us -> none
where the time goes in v4:
time: 51.1 us; the launch traced here: 51 us
  Pallas kernels  50.3 us (98%)
  between operations  0.64 us (1%)
    pallas_call x1, Pallas kernels, local(): pl.pallas_call(kernel, out_shape=(pltpu.VMEM((4, 2, ROWS, LANES), F32), p...  49 us
    pallas_call x1, Pallas kernels, local(): pl.pallas_call(unpack_kernel, out_shape=(jax.ShapeDtypeStruct((BRICK, ROW...  1.31 us

profile of v4, /device:TPU:0, one launch (start us, length us, event | category | flops | bytes accessed | tf_op | source)
XLA Modules:
  0.0 51.0 jit_solution(15454230089864607299)
XLA Ops:
  0.6 49.0 %shard_map.68 = (f32[4,2,32,128]{3,2,1,0:T(8,128)S(1)}, f32[8,128]{1,0:T(8,128)S(1)}) custom-call(f32[1024,32]{1,0:T(8,128)} %bitcast.5, f32[1024,32]{1,0:T(8,128)} %bitcast.6, f32[1024,32]{1,0:T(8,128)} %bitcast.7, f32[26]{0:T(128)} %w_hbm.1, f32[32]{0:T(128)} %om_hbm.1), custom_call_target="tpu_custom_call" | custom-call | tf_op jit(solution)/shard_map/pallas_call | solution.py:341
  49.7 1.3 %shard_map.69 = (f32[1024,32]{1,0:T(8,128)}, f32[1,32]{1,0:T(1,128)}) custom-call(f32[4,2,32,128]{3,2,1,0:T(8,128)S(1)} %get-tuple-element.6.dense_ref, f32[8,128]{1,0:T(8,128)S(1)} %get-tuple-element.7.total_ref), custom_call_target="tpu_custom_call" | custom-call | tf_op jit(solution)/shard_map/pallas_call | solution.py:370

commit v5 on v4

--- a/solution.py
+++ b/solution.py
@@ -9,12 +9,18 @@
 F32 = jnp.float32
 ROWS = 32
 LANES = 128
-BRICK = 1024
+MIB = 1024 * 1024
+PITCH = 40
+PITCHED = ROWS * PITCH
 DEPTH = 8
 BLOCKS = 4
 CELLS = 64 * 64 * 64
 OFFSETS = [(a, b, c) for a in (-1, 0, 1) for b in (-1, 0, 1) for c in (-1, 0, 1) if (a, b, c) != (0, 0, 0)]
 TERM = {o: n for n, o in enumerate(OFFSETS)}
+
+
+def rows_of(ref):
+    return ref.reshape(ROWS, PITCH, ROWS).at[:, pl.ds(0, ROWS), :]
 
 
 def kernel(u_ref, f_ref, k_ref, w_hbm, om_hbm, out_ref, rho_ref,
@@ -25,12 +31,12 @@
     zc = lax.axis_index('z')
     me = 4 * zc + 2 * yc + xc
     turn = (yc + zc) % 2
-    my_l = xc + turn * (3 - 2 * xc)
+    my_l = xc + 2 * turn
     my_q = 2 * xc + zc
 
     def slab_device(slab_y, slab_l):
         t = slab_l // 2
-        return {'batch': 0, 'z': (slab_y + t) % 2, 'y': slab_y, 'x': slab_l + t * (3 - 2 * slab_l)}
+        return {'batch': 0, 'z': (slab_y + t) % 2, 'y': slab_y, 'x': slab_l % 2}
 
     def ring_device(step):
         s = (4 * yc + my_l + step + 8) % 8
@@ -43,26 +49,32 @@
     top = lax.broadcasted_iota(jnp.int32, (1, 8, LANES), 1) == 0
     lane_in = lax.broadcasted_iota(jnp.int32, (LANES, LANES), 0)
     lane_out = lax.broadcasted_iota(jnp.int32, (LANES, LANES), 1)
-    weave = (lane_out == 2 * (lane_in % 64) + lane_in // 64).astype(F32)
-    unweave = (lane_in == 2 * (lane_out % 64) + lane_out // 64).astype(F32)
+    weave = (lane_out == 2 * (lane_in % 64) + lane_in // 64).astype(F32).astype(jnp.bfloat16)
+    unweave = (lane_in == 2 * (lane_out % 64) + lane_out // 64).astype(F32).astype(jnp.bfloat16)
 
     def move_lanes(v, matrix):
-        return jnp.dot(v, matrix, precision=lax.Precision.HIGHEST, preferred_element_type=F32)
-
-    barrier = pltpu.get_barrier_semaphore()
-    for r in range(1, 8):
-        pl.semaphore_signal(barrier, inc=1, device_id=device((me + r) % 8), device_id_type=MESH)
-
-    loads = [pltpu.make_async_copy(ref, bricks.at[a], brick_sem.at[a]) for a, ref in enumerate((k_ref, u_ref, f_ref))]
+        total = None
+        for _ in range(3):
+            part = v.astype(jnp.bfloat16)
+            v = v - part.astype(F32)
+            moved = jnp.dot(part, matrix, preferred_element_type=F32)
+            total = moved if total is None else total + moved
+        return total
+
+    loads = [pltpu.make_async_copy(ref, rows_of(bricks.at[pl.ds(a * PITCHED, PITCHED)]), brick_sem.at[a]) for a, ref in enumerate((k_ref, u_ref, f_ref))]
     loads.append(pltpu.make_async_copy(w_hbm, w_ref, brick_sem.at[3]))
     loads.append(pltpu.make_async_copy(om_hbm, om_ref, brick_sem.at[4]))
     for load in loads:
         load.start()
 
+    barrier = pltpu.get_barrier_semaphore()
+    for r in range(1, 8):
+        pl.semaphore_signal(barrier, inc=1, device_id=device((me + r) % 8), device_id_type=MESH)
+
     def pack_array(a):
         loads[a].wait()
         for i in range(8):
-            rows = [bricks[a, pl.ds(4 * i + m, ROWS, stride=ROWS), :] for m in range(4)]
+            rows = [bricks[pl.ds(a * PITCHED + 4 * i + m, ROWS, stride=PITCH), :] for m in range(4)]
             pack[a, i] = jnp.concatenate(rows, axis=1)
 
     def own_copy(a, r):
@@ -100,10 +112,9 @@
             own_copy(a, r).wait_recv()
 
     def unpack_own(a, store):
-        for yy in range(2):
-            for m in range(4):
-                v = jnp.concatenate([recv_own[a, q, yy, :, ROWS * m:ROWS * m + ROWS] for q in range(4)], axis=1)
-                store(4 * yy + m, move_lanes(v, weave))
+        planes = [jnp.concatenate([recv_own[a, q, yy, :, ROWS * m:ROWS * m + ROWS] for q in range(4)], axis=1)
+                  for yy in range(2) for m in range(4)]
+        store(move_lanes(jnp.concatenate(planes, axis=0), weave).reshape(8, ROWS, LANES))
 
     def ring_copy(e, src, dst, side, part):
         first = 4 * (1 - part) if side == 0 else 4 * part
@@ -141,14 +152,14 @@
     send_own(2)
 
     wait_own(0)
-    unpack_own(0, lambda y, v: put(kap, 8 + y, v[None]))
+    unpack_own(0, lambda v: put(kap, 8, v))
     for side in range(2):
         kap_copy(side, 0).start()
     wait_own(1)
 
-    def store_u(y, v):
-        stage[y] = v
-        put(fld, 8 + y, v[None])
+    def store_u(v):
+        stage[...] = v
+        put(fld, 8, v)
     unpack_own(1, store_u)
     for side in range(2):
         u_copy(2, side, 0).start()
@@ -156,8 +167,8 @@
         kap_copy(side, 1).start()
     wait_own(2)
 
-    def store_f(y, v):
-        src_own[8 + y] = v
+    def store_f(v):
+        src_own[8:16] = v
     unpack_own(2, store_f)
     for side in range(2):
         f_copy(side, 0).start()
@@ -292,8 +303,9 @@
             src_ref=back.at[q], dst_ref=back_recv.at[my_l], send_sem=back_send.at[r - 1], recv_sem=back_recv_sem.at[r - 1],
             device_id={'batch': 0, 'z': q % 2, 'y': yc, 'x': q // 2}, device_id_type=MESH)
 
+    planes8 = move_lanes(stage[...].reshape(8 * ROWS, LANES), unweave).reshape(8, ROWS, LANES)
     for yy in range(2):
-        planes = [move_lanes(fld[8 + 4 * yy + m, row(1, 8), :], unweave) for m in range(4)]
+        planes = [planes8[4 * yy + m] for m in range(4)]
         for q in range(4):
             back[q, yy] = jnp.concatenate([v[:, ROWS * q:ROWS * q + ROWS] for v in planes], axis=1)
     for r in range(1, 4):
@@ -346,7 +358,7 @@
             scratch_shapes=[
                 pltpu.SMEM((26,), F32),
                 pltpu.SMEM((ROWS,), F32),
-                pltpu.VMEM((3, BRICK, ROWS), F32),
+                pltpu.VMEM((3 * PITCHED, ROWS), F32),
                 dma((5,)),
                 pltpu.VMEM((3, 8, ROWS, LANES), F32),
                 pltpu.VMEM((3, 4, 2, ROWS, LANES), F32),
@@ -365,14 +377,14 @@
                 pltpu.VMEM((4, 2, ROWS, LANES), F32),
                 dma((3, 3)), dma((3, 3)), dma((6, 2, 2)), dma((6, 2, 2)), dma((3,)), dma((3,)), dma((7,)), dma((7,)),
             ],
-            compiler_params=pltpu.CompilerParams(collective_id=0, has_side_effects=True, vmem_limit_bytes=60 * BRICK * BRICK),
-        )(u.reshape(BRICK, ROWS), f.reshape(BRICK, ROWS), kappa.reshape(BRICK, ROWS), w, om)
+            compiler_params=pltpu.CompilerParams(collective_id=0, has_side_effects=True, vmem_limit_bytes=60 * MIB),
+        )(u, f, kappa, w, om)
         out, rho = pl.pallas_call(
             unpack_kernel,
-            out_shape=(jax.ShapeDtypeStruct((BRICK, ROWS), F32), jax.ShapeDtypeStruct((1, ROWS), F32)),
+            out_shape=(jax.ShapeDtypeStruct((ROWS * ROWS, ROWS), F32), jax.ShapeDtypeStruct((1, ROWS), F32)),
             in_specs=[vmem, vmem],
             out_specs=(vmem, vmem),
-            compiler_params=pltpu.CompilerParams(vmem_limit_bytes=8 * BRICK * BRICK),
+            compiler_params=pltpu.CompilerParams(vmem_limit_bytes=8 * MIB),
         )(dense, total)
         return out.reshape(ROWS, ROWS, ROWS), rho.reshape(ROWS)
 

time: 51.1 us -> 49.6 us (0.971)
  Pallas kernels: 50.3 us -> 48.9 us
    pallas_call x1, Pallas kernels: 49 us -> 47.5 us  [local(): pl.pallas_call(kernel, out_shape=(pltpu.VMEM((4, 2, ROWS, LANES), F32), p...]
where the time goes in v5:
time: 49.6 us; the launch traced here: 49.5 us
  Pallas kernels  48.9 us (99%)
  between operations  0.64 us (1%)
    pallas_call x1, Pallas kernels, local(): pl.pallas_call(kernel, out_shape=(pltpu.VMEM((4, 2, ROWS, LANES), F32), p...  47.5 us
    pallas_call x1, Pallas kernels, local(): pl.pallas_call(unpack_kernel, out_shape=(jax.ShapeDtypeStruct((ROWS * ROW...  1.31 us

profile of v5, /device:TPU:0, one launch (start us, length us, event | category | flops | bytes accessed | tf_op | source)
XLA Modules:
  0.0 49.5 jit_solution(10574158310921492560)
XLA Ops:
  0.6 47.5 %shard_map.68 = (f32[4,2,32,128]{3,2,1,0:T(8,128)S(1)}, f32[8,128]{1,0:T(8,128)S(1)}) custom-call(f32[32,32,32]{2,1,0:T(8,128)} %u_ref.1, f32[32,32,32]{2,1,0:T(8,128)} %f_ref.1, f32[32,32,32]{2,1,0:T(8,128)} %k_ref.1, f32[26]{0:T(128)} %w_hbm.1, f32[32]{0:T(128)} %om_hbm.1), custom_call_target="tpu_custom_call" | custom-call | tf_op jit(solution)/shard_map/pallas_call | solution.py:353
  48.2 1.3 %shard_map.69 = (f32[1024,32]{1,0:T(8,128)}, f32[1,32]{1,0:T(1,128)}) custom-call(f32[4,2,32,128]{3,2,1,0:T(8,128)S(1)} %get-tuple-element.6.dense_ref, f32[8,128]{1,0:T(8,128)S(1)} %get-tuple-element.7.total_ref), custom_call_target="tpu_custom_call" | custom-call | tf_op jit(solution)/shard_map/pallas_call | solution.py:382

commit v6 on v5

--- a/solution.py
+++ b/solution.py
@@ -116,12 +116,15 @@
                   for yy in range(2) for m in range(4)]
         store(move_lanes(jnp.concatenate(planes, axis=0), weave).reshape(8, ROWS, LANES))
 
+    def part_start(side, part):
+        return 4 * (1 - part) * (1 - side) + 4 * part * side
+
     def ring_copy(e, src, dst, side, part):
-        first = 4 * (1 - part) if side == 0 else 4 * part
+        first = part_start(side, part)
         return pltpu.make_async_remote_copy(
             src_ref=src(first), dst_ref=dst(side, first),
             send_sem=ring_send.at[e, side, part], recv_sem=ring_recv.at[e, side, part],
-            device_id=ring_device(1 if side == 0 else -1), device_id_type=MESH)
+            device_id=ring_device(1 - 2 * side), device_id_type=MESH)
 
     def halo_dst(e):
         return lambda side, first: halo.at[e, side, pl.ds(first, 4)]
@@ -138,10 +141,9 @@
 
     PARTS = [(side, part) for part in range(2) for side in range(2)]
 
-    def unpack_halo(e, dst, part):
-        for side in range(2):
-            j = 4 * (1 - part) if side == 0 else 4 * part
-            put(dst, 16 * side + j, halo[e, side, j:j + 4])
+    def unpack_side(e, dst, side, part):
+        j = part_start(side, part)
+        put(dst, 16 * side + j, halo[e, side, pl.ds(j, 4)])
 
     pack_array(0)
     pl.semaphore_wait(barrier, 7)
@@ -215,74 +217,96 @@
     for part in range(2):
         for side in range(2):
             kap_copy(side, part).wait()
-        unpack_halo(0, kap, part)
+            unpack_side(0, kap, side, part)
         coef_range(*((5, 9) if part == 0 else (1, 5)))
         coef_range(*((15, 19) if part == 0 else (19, 23)))
-
-    def pair(level, first, second, n, before, blk):
-        src, dst = (0, 24) if level % 2 == 1 else (24, 0)
+    scale_range(8, 9)
+    scale_range(15, 16)
+
+    def strip(level, left, n, right, before, blk, final=False):
+        src = 24 * ((level + 1) % 2)
+        dst = 24 - src
+        lo = left + right * (24 - n - 2 * left)
         k = DEPTH * blk + level - 1
-        om = om_ref[k]
-        owned = first + n > 8
-
-        def body(s, _):
-            lo = first + s * (second - first)
-            last = before + s * (dst + first - before)
-            turned = fld[pl.ds(last, 4), row(1, 8), :]
-            center = fld[pl.ds(src + lo, n), row(1, 8), :]
-            acc = src_div[pl.ds(lo, n)] - center
-            for ox in (-1, 0, 1):
-                for oz in (-1, 0, 1):
-                    near = fld[pl.ds(src + lo - 1, n + 2), row(oz + 1, 8 + ox), :]
-                    for oy in (-1, 0, 1):
-                        if (ox, oy, oz) != (0, 0, 0):
-                            t = 40 * TERM[(ox, oy, oz)]
-                            acc = acc + coef[pl.ds(lo, n), t:t + ROWS, :] * near[1 + oy:1 + oy + n]
-            new = center + om * acc
-            fld[pl.ds(dst + lo, n), row(1, 8), :] = new
-            put_turned(fld, last, turned)
-            if level == DEPTH:
-                stage[pl.ds(lo - 8, n)] = new
-            if owned:
-                r = acc * diag[pl.ds(lo, n)]
-                r = jnp.sum(r * r, axis=0)
-                sums[k] = sums[k] + ((r[0:8] + r[8:16]) + (r[16:24] + r[24:ROWS]))
-            return 0
-        if first == second:
-            body(0, 0)
-        else:
-            lax.fori_loop(0, 2, body, 0)
-        return dst + second
+        turned = fld[pl.ds(before, 4), row(1, 8), :]
+        center = fld[pl.ds(src + lo, n), row(1, 8), :]
+        acc = src_div[pl.ds(lo, n)] - center
+        for ox in (-1, 0, 1):
+            for oz in (-1, 0, 1):
+                near = fld[pl.ds(src + lo - 1, n + 2), row(oz + 1, 8 + ox), :]
+                for oy in (-1, 0, 1):
+                    if (ox, oy, oz) != (0, 0, 0):
+                        t = 40 * TERM[(ox, oy, oz)]
+                        acc = acc + coef[pl.ds(lo, n), t:t + ROWS, :] * near[1 + oy:1 + oy + n]
+        new = center + om_ref[k] * acc
+        fld[pl.ds(dst + lo, n), row(1, 8), :] = new
+        put_turned(fld, before, turned)
+        if final:
+            stage[pl.ds(lo - 8, n)] = new
+        r = acc * diag[pl.ds(lo, n)]
+        r = jnp.sum(r * r, axis=0)
+        sums[k] = sums[k] + ((r[0:8] + r[8:16]) + (r[16:24] + r[24:32]))
+        return dst + lo
 
     def flush(before):
         put_turned(fld, before, fld[pl.ds(before, 4), row(1, 8), :])
         return before
 
+    fast = 1 - xc
+    slow = xc
+
+    def fast_pass(t, before, blk):
+        level = 1 + t // 2
+        return strip(level, level + 4 * (1 - t % 2), 4, fast, before, blk)
+
     def block(blk, _):
         e = 2 + blk
-        before = 8
-        for level, first, second, n in ((1, 9, 12, 3), (2, 10, 10, 4), (3, 11, 11, 2)):
-            before = flush(pair(level, first, second, n, before, blk))
+        before = strip(1, 9, 3, 0, 8, blk)
+        before = flush(strip(1, 9, 3, 1, before, blk))
+        before = flush(strip(2, 10, 4, 0, before, blk))
+        before = flush(strip(3, 11, 2, 0, before, blk))
+
+        @pl.when(blk == 0)
+        def _():
+            for part in range(2):
+                f_copy(fast, part).wait_recv()
+            scale_range(1 + 15 * fast, 8 + 15 * fast)
         for part in range(2):
-            @pl.when(blk == 0)
-            def _():
-                left, right = (5, 15) if part == 0 else (1, 19)
-                for side in range(2):
-                    f_copy(side, part).wait()
-                scale_range(left, left + 4)
-                scale_range(right, right + 4)
-            for side in range(2):
-                u_copy(e, side, part).wait()
-            unpack_halo(e, fld, part)
-            if part == 0:
-                for level in range(1, 4):
-                    before = pair(level, 4 + level, 16 - level, 4, before, blk)
-            else:
-                for level in range(1, 9):
-                    before = pair(level, level, 20 - level, 4, before, blk)
-                    if level < 5:
-                        first, second, n = ((8, 12, 4), (9, 12, 3), (10, 10, 4), (11, 11, 2))[level - 1]
-                        before = pair(3 + level, first, second, n, before, blk)
+            u_copy(e, fast, part).wait_recv()
+        for part in range(2):
+            unpack_side(e, fld, fast, part)
+        before = lax.fori_loop(0, 8, lambda t, b: fast_pass(t, b, blk), before)
+
+        @pl.when(blk == 0)
+        def _():
+            f_copy(slow, 0).wait_recv()
+            scale_range(4 + 12 * slow, 8 + 12 * slow)
+        u_copy(e, slow, 0).wait_recv()
+        unpack_side(e, fld, slow, 0)
+        before = lax.fori_loop(0, 2, lambda s, b: strip(1 + 4 * s, 5, 4, slow + s * (fast - slow), b, blk), before)
+        before = flush(strip(2, 6, 4, slow, before, blk))
+        before = strip(3, 7, 4, slow, before, blk)
+
+        @pl.when(blk == 0)
+        def _():
+            f_copy(slow, 1).wait_recv()
+            scale_range(1 + 19 * slow, 4 + 19 * slow)
+            for side, part in PARTS:
+                f_copy(side, part).wait_send()
+        u_copy(e, slow, 1).wait_recv()
+        for side, part in PARTS:
+            u_copy(e, side, part).wait_send()
+        unpack_side(e, fld, slow, 1)
+        before = lax.fori_loop(0, 2, lambda s, b: strip(1 + 3 * s, 1 + 7 * s, 4, slow, b, blk), before)
+        before = strip(2, 2, 4, slow, before, blk)
+        before = lax.fori_loop(0, 2, lambda s, b: strip(5, 9, 3, s, b, blk), before)
+        before = lax.fori_loop(0, 2, lambda s, b: strip(3 + 3 * s, 3 + 7 * s, 4, slow, b, blk), before)
+        before = strip(4, 4, 4, slow, before, blk)
+        before = strip(7, 11, 2, 0, before, blk)
+        before = strip(5, 5, 4, slow, before, blk)
+        before = lax.fori_loop(
+            0, 4, lambda t, b: strip(6 + t // 2, 6 + t // 2, 4, fast + (t % 2) * (slow - fast), b, blk), before)
+        before = lax.fori_loop(0, 2, lambda s, b: strip(8, 8, 4, fast + s * (slow - fast), b, blk, True), before)
 
         @pl.when(blk < BLOCKS - 1)
         def _():

time: 49.6 us -> 46.8 us (0.944)
  Pallas kernels: 48.9 us -> 46.1 us
    pallas_call x1, Pallas kernels: 47.5 us -> 44.8 us  [local(): pl.pallas_call(kernel, out_shape=(pltpu.VMEM((4, 2, ROWS, LANES), F32), p...]
where the time goes in v6:
time: 46.8 us; the launch traced here: 46.7 us
  Pallas kernels  46.1 us (99%)
  between operations  0.64 us (1%)
    pallas_call x1, Pallas kernels, local(): pl.pallas_call(kernel, out_shape=(pltpu.VMEM((4, 2, ROWS, LANES), F32), p...  44.8 us
    pallas_call x1, Pallas kernels, local(): pl.pallas_call(unpack_kernel, out_shape=(jax.ShapeDtypeStruct((ROWS * ROW...  1.31 us

profile of v6, /device:TPU:0, one launch (start us, length us, event | category | flops | bytes accessed | tf_op | source)
XLA Modules:
  0.0 46.7 jit_solution(13902145083350810127)
XLA Ops:
  0.6 44.8 %shard_map.68 = (f32[4,2,32,128]{3,2,1,0:T(8,128)S(1)}, f32[8,128]{1,0:T(8,128)S(1)}) custom-call(f32[32,32,32]{2,1,0:T(8,128)} %u_ref.1, f32[32,32,32]{2,1,0:T(8,128)} %f_ref.1, f32[32,32,32]{2,1,0:T(8,128)} %k_ref.1, f32[26]{0:T(128)} %w_hbm.1, f32[32]{0:T(128)} %om_hbm.1), custom_call_target="tpu_custom_call" | custom-call | tf_op jit(solution)/shard_map/pallas_call | solution.py:377
  45.4 1.3 %shard_map.69 = (f32[1024,32]{1,0:T(8,128)}, f32[1,32]{1,0:T(1,128)}) custom-call(f32[4,2,32,128]{3,2,1,0:T(8,128)S(1)} %get-tuple-element.6.dense_ref, f32[8,128]{1,0:T(8,128)S(1)} %get-tuple-element.7.total_ref), custom_call_target="tpu_custom_call" | custom-call | tf_op jit(solution)/shard_map/pallas_call | solution.py:406

commit v7 on v6

--- a/solution.py
+++ b/solution.py
@@ -34,6 +34,9 @@
     my_l = xc + 2 * turn
     my_q = 2 * xc + zc
 
+    fast = 1 - xc
+    slow = xc
+
     def slab_device(slab_y, slab_l):
         t = slab_l // 2
         return {'batch': 0, 'z': (slab_y + t) % 2, 'y': slab_y, 'x': slab_l % 2}
@@ -155,29 +158,29 @@
 
     wait_own(0)
     unpack_own(0, lambda v: put(kap, 8, v))
-    for side in range(2):
-        kap_copy(side, 0).start()
+    kap_copy(fast, 0).start()
+    for part in range(2):
+        kap_copy(slow, part).start()
     wait_own(1)
 
     def store_u(v):
         stage[...] = v
         put(fld, 8, v)
     unpack_own(1, store_u)
-    for side in range(2):
-        u_copy(2, side, 0).start()
-    for side in range(2):
-        kap_copy(side, 1).start()
+    u_copy(2, fast, 0).start()
+    for part in range(2):
+        u_copy(2, slow, part).start()
+    kap_copy(fast, 1).start()
     wait_own(2)
 
     def store_f(v):
         src_own[8:16] = v
     unpack_own(2, store_f)
-    for side in range(2):
-        f_copy(side, 0).start()
-    for side in range(2):
-        u_copy(2, side, 1).start()
-    for side in range(2):
-        f_copy(side, 1).start()
+    f_copy(fast, 0).start()
+    for part in range(2):
+        f_copy(slow, part).start()
+    u_copy(2, fast, 1).start()
+    f_copy(fast, 1).start()
 
     loads[3].wait()
     loads[4].wait()
@@ -215,13 +218,17 @@
     coef_range(9, 15)
     scale_range(9, 15)
     for part in range(2):
-        for side in range(2):
-            kap_copy(side, part).wait()
-            unpack_side(0, kap, side, part)
-        coef_range(*((5, 9) if part == 0 else (1, 5)))
-        coef_range(*((15, 19) if part == 0 else (19, 23)))
-    scale_range(8, 9)
-    scale_range(15, 16)
+        kap_copy(fast, part).wait_recv()
+        unpack_side(0, kap, fast, part)
+    coef_range(1 + 14 * fast, 9 + 14 * fast)
+
+    def slow_setup(part, left):
+        lo = left + slow * (20 - 2 * left)
+        kap_copy(slow, part).wait_recv()
+        unpack_side(0, kap, slow, part)
+        coef_range(lo, lo + 4)
+        f_copy(slow, part).wait_recv()
+        scale_range(lo, lo + 4)
 
     def strip(level, left, n, right, before, blk, final=False):
         src = 24 * ((level + 1) % 2)
@@ -252,9 +259,6 @@
         put_turned(fld, before, fld[pl.ds(before, 4), row(1, 8), :])
         return before
 
-    fast = 1 - xc
-    slow = xc
-
     def fast_pass(t, before, blk):
         level = 1 + t // 2
         return strip(level, level + 4 * (1 - t % 2), 4, fast, before, blk)
@@ -270,7 +274,7 @@
         def _():
             for part in range(2):
                 f_copy(fast, part).wait_recv()
-            scale_range(1 + 15 * fast, 8 + 15 * fast)
+            scale_range(1 + 14 * fast, 9 + 14 * fast)
         for part in range(2):
             u_copy(e, fast, part).wait_recv()
         for part in range(2):
@@ -279,8 +283,7 @@
 
         @pl.when(blk == 0)
         def _():
-            f_copy(slow, 0).wait_recv()
-            scale_range(4 + 12 * slow, 8 + 12 * slow)
+            slow_setup(0, 5)
         u_copy(e, slow, 0).wait_recv()
         unpack_side(e, fld, slow, 0)
         before = lax.fori_loop(0, 2, lambda s, b: strip(1 + 4 * s, 5, 4, slow + s * (fast - slow), b, blk), before)
@@ -289,9 +292,9 @@
 
         @pl.when(blk == 0)
         def _():
-            f_copy(slow, 1).wait_recv()
-            scale_range(1 + 19 * slow, 4 + 19 * slow)
+            slow_setup(1, 1)
             for side, part in PARTS:
+                kap_copy(side, part).wait_send()
                 f_copy(side, part).wait_send()
         u_copy(e, slow, 1).wait_recv()
         for side, part in PARTS:
@@ -310,8 +313,9 @@
 
         @pl.when(blk < BLOCKS - 1)
         def _():
-            for side, part in PARTS:
-                u_copy(e + 1, side, part).start()
+            for side in (fast, slow):
+                for part in range(2):
+                    u_copy(e + 1, side, part).start()
             flush(before)
         return 0
     lax.fori_loop(0, BLOCKS, block, 0)

time: 46.8 us -> 45.7 us (0.976)
  Pallas kernels: 46.1 us -> 44.9 us
    pallas_call x1, Pallas kernels: 44.8 us -> 43.6 us  [local(): pl.pallas_call(kernel, out_shape=(pltpu.VMEM((4, 2, ROWS, LANES), F32), p...]
where the time goes in v7:
time: 45.7 us; the launch traced here: 45.5 us
  Pallas kernels  44.9 us (98%)
  between operations  0.64 us (1%)
    pallas_call x1, Pallas kernels, local(): pl.pallas_call(kernel, out_shape=(pltpu.VMEM((4, 2, ROWS, LANES), F32), p...  43.6 us
    pallas_call x1, Pallas kernels, local(): pl.pallas_call(unpack_kernel, out_shape=(jax.ShapeDtypeStruct((ROWS * ROW...  1.31 us

profile of v7, /device:TPU:0, one launch (start us, length us, event | category | flops | bytes accessed | tf_op | source)
XLA Modules:
  0.0 45.5 jit_solution(1268223952694161581)
XLA Ops:
  0.6 43.6 %shard_map.68 = (f32[4,2,32,128]{3,2,1,0:T(8,128)S(1)}, f32[8,128]{1,0:T(8,128)S(1)}) custom-call(f32[32,32,32]{2,1,0:T(8,128)} %u_ref.1, f32[32,32,32]{2,1,0:T(8,128)} %f_ref.1, f32[32,32,32]{2,1,0:T(8,128)} %k_ref.1, f32[26]{0:T(128)} %w_hbm.1, f32[32]{0:T(128)} %om_hbm.1), custom_call_target="tpu_custom_call" | custom-call | tf_op jit(solution)/shard_map/pallas_call | solution.py:381
  44.2 1.3 %shard_map.69 = (f32[1024,32]{1,0:T(8,128)}, f32[1,32]{1,0:T(1,128)}) custom-call(f32[4,2,32,128]{3,2,1,0:T(8,128)S(1)} %get-tuple-element.6.dense_ref, f32[8,128]{1,0:T(8,128)S(1)} %get-tuple-element.7.total_ref), custom_call_target="tpu_custom_call" | custom-call | tf_op jit(solution)/shard_map/pallas_call | solution.py:410

commit v8 on v7

--- a/solution.py
+++ b/solution.py
@@ -45,8 +45,11 @@
         s = (4 * yc + my_l + step + 8) % 8
         return slab_device(s // 4, s % 4)
 
-    def device(i):
-        return {'batch': 0, 'z': i // 4, 'y': (i // 2) % 2, 'x': i % 2}
+    def flip(bit, swap):
+        return 1 - bit if swap else bit
+
+    def partner(r):
+        return {'batch': 0, 'z': flip(zc, r & 2), 'y': flip(yc, r & 4), 'x': flip(xc, r & 1)}
 
     even = lax.broadcasted_iota(jnp.int32, (1, 8, LANES), 2) % 2 == 0
     top = lax.broadcasted_iota(jnp.int32, (1, 8, LANES), 1) == 0
@@ -72,7 +75,7 @@
 
     barrier = pltpu.get_barrier_semaphore()
     for r in range(1, 8):
-        pl.semaphore_signal(barrier, inc=1, device_id=device((me + r) % 8), device_id_type=MESH)
+        pl.semaphore_signal(barrier, inc=1, device_id=partner(r), device_id_type=MESH)
 
     def pack_array(a):
         loads[a].wait()
@@ -81,11 +84,11 @@
             pack[a, i] = jnp.concatenate(rows, axis=1)
 
     def own_copy(a, r):
-        dest = (my_l + r) % 4
+        dest = flip(xc, r & 1) + 2 * flip(turn, r & 2)
         return pltpu.make_async_remote_copy(
             src_ref=pack.at[a, pl.ds(2 * dest, 2)], dst_ref=recv_own.at[a, my_q],
             send_sem=own_send.at[a, r - 1], recv_sem=own_recv.at[a, r - 1],
-            device_id=slab_device(yc, dest), device_id_type=MESH)
+            device_id=partner(r), device_id_type=MESH)
 
     def send_own(a):
         for r in range(1, 4):
@@ -140,7 +143,7 @@
                          lambda side, first: src_own.at[pl.ds(16 * side + first, 4)], side, part)
 
     def u_copy(e, side, part):
-        return ring_copy(e, lambda first: stage.at[pl.ds(first, 4)], halo_dst(e), side, part)
+        return ring_copy(e, lambda first: stage.at[pl.ds(first, 4), pl.ds(0, ROWS), :], halo_dst(e), side, part)
 
     PARTS = [(side, part) for part in range(2) for side in range(2)]
 
@@ -164,7 +167,7 @@
     wait_own(1)
 
     def store_u(v):
-        stage[...] = v
+        stage[:, 0:ROWS, :] = v
         put(fld, 8, v)
     unpack_own(1, store_u)
     u_copy(2, fast, 0).start()
@@ -236,11 +239,13 @@
         lo = left + right * (24 - n - 2 * left)
         k = DEPTH * blk + level - 1
         turned = fld[pl.ds(before, 4), row(1, 8), :]
-        center = fld[pl.ds(src + lo, n), row(1, 8), :]
-        acc = src_div[pl.ds(lo, n)] - center
-        for ox in (-1, 0, 1):
-            for oz in (-1, 0, 1):
+        acc = src_div[pl.ds(lo, n)]
+        for ox in (0, -1, 1):
+            for oz in (0, -1, 1):
                 near = fld[pl.ds(src + lo - 1, n + 2), row(oz + 1, 8 + ox), :]
+                if (ox, oz) == (0, 0):
+                    center = near[1:1 + n]
+                    acc = acc - center
                 for oy in (-1, 0, 1):
                     if (ox, oy, oz) != (0, 0, 0):
                         t = 40 * TERM[(ox, oy, oz)]
@@ -249,7 +254,7 @@
         fld[pl.ds(dst + lo, n), row(1, 8), :] = new
         put_turned(fld, before, turned)
         if final:
-            stage[pl.ds(lo - 8, n)] = new
+            stage[pl.ds(lo - 8, n), 0:ROWS, :] = new
         r = acc * diag[pl.ds(lo, n)]
         r = jnp.sum(r * r, axis=0)
         sums[k] = sums[k] + ((r[0:8] + r[8:16]) + (r[16:24] + r[24:32]))
@@ -323,21 +328,24 @@
     def sum_copy(r):
         return pltpu.make_async_remote_copy(
             src_ref=psum.at[8], dst_ref=psum.at[me], send_sem=sum_send.at[r - 1], recv_sem=sum_recv.at[r - 1],
-            device_id=device((me + r) % 8), device_id_type=MESH)
-
-    def back_copy(r):
-        q = (my_q + r) % 4
+            device_id=partner(r), device_id_type=MESH)
+
+    def back_copy(r, yy):
+        q = 2 * flip(xc, r & 1) + flip(zc, r & 2)
         return pltpu.make_async_remote_copy(
-            src_ref=back.at[q], dst_ref=back_recv.at[my_l], send_sem=back_send.at[r - 1], recv_sem=back_recv_sem.at[r - 1],
-            device_id={'batch': 0, 'z': q % 2, 'y': yc, 'x': q // 2}, device_id_type=MESH)
-
-    planes8 = move_lanes(stage[...].reshape(8 * ROWS, LANES), unweave).reshape(8, ROWS, LANES)
+            src_ref=back.at[q, yy], dst_ref=back_recv.at[my_l, yy],
+            send_sem=back_send.at[yy, r - 1], recv_sem=back_recv_sem.at[yy, r - 1],
+            device_id=partner(r), device_id_type=MESH)
+
+    flat_stage = stage.reshape(8 * PITCH, LANES)
     for yy in range(2):
-        planes = [planes8[4 * yy + m] for m in range(4)]
+        tiles = [flat_stage[pl.ds(16 * yy + x, 8, stride=PITCH), :] for x in range(16)]
+        tiles = move_lanes(jnp.concatenate(tiles, axis=0), unweave).reshape(4, 4, 8, LANES)
         for q in range(4):
-            back[q, yy] = jnp.concatenate([v[:, ROWS * q:ROWS * q + ROWS] for v in planes], axis=1)
-    for r in range(1, 4):
-        back_copy(r).start()
+            quarter = [tiles[:, m, :, ROWS * q:ROWS * q + ROWS] for m in range(4)]
+            back[q, yy] = jnp.concatenate(quarter, axis=2).reshape(ROWS, LANES)
+        for r in range(1, 4):
+            back_copy(r, yy).start()
     back_recv[my_l] = back[my_q]
     flat = jnp.sum(sums[...], axis=1)
     flat = jnp.concatenate([flat, jnp.zeros((96, LANES), F32)], axis=0)
@@ -349,7 +357,8 @@
         sum_copy(r).start()
 
     for r in range(1, 4):
-        back_copy(r).wait()
+        for yy in range(2):
+            back_copy(r, yy).wait()
     out_ref[...] = back_recv[...]
     for r in range(1, 8):
         sum_copy(r).wait()
@@ -364,10 +373,11 @@
 
 
 def unpack_kernel(dense_ref, total_ref, out_ref, rho_ref):
-    for i in range(8):
-        v = dense_ref[i // 2, i % 2]
-        for m in range(4):
-            out_ref[pl.ds(4 * i + m, ROWS, stride=ROWS), :] = v[:, ROWS * m:ROWS * m + ROWS]
+    for slab in range(4):
+        for x in range(ROWS):
+            i, m = x % 16 // 4, ROWS * (x % 4)
+            first = ROWS * x + 8 * slab
+            out_ref[first:first + 8, :] = dense_ref[slab, x // 16, 8 * i:8 * i + 8, m:m + ROWS]
     rho_ref[...] = jnp.sqrt(total_ref[...] / CELLS)[0:1, 0:ROWS]
 
 
@@ -397,13 +407,13 @@
                 pltpu.VMEM((24, ROWS, LANES), F32),
                 pltpu.VMEM((24, ROWS, LANES), F32),
                 pltpu.VMEM((24, ROWS, LANES), F32),
-                pltpu.VMEM((8, ROWS, LANES), F32),
+                pltpu.VMEM((8, PITCH, LANES), F32),
                 pltpu.VMEM((6, 2, 8, ROWS, LANES), F32),
                 pltpu.VMEM((ROWS, 8, LANES), F32),
                 pltpu.VMEM((9, 8, LANES), F32),
                 pltpu.VMEM((4, 2, ROWS, LANES), F32),
                 pltpu.VMEM((4, 2, ROWS, LANES), F32),
-                dma((3, 3)), dma((3, 3)), dma((6, 2, 2)), dma((6, 2, 2)), dma((3,)), dma((3,)), dma((7,)), dma((7,)),
+                dma((3, 3)), dma((3, 3)), dma((6, 2, 2)), dma((6, 2, 2)), dma((2, 3)), dma((2, 3)), dma((7,)), dma((7,)),
             ],
             compiler_params=pltpu.CompilerParams(collective_id=0, has_side_effects=True, vmem_limit_bytes=60 * MIB),
         )(u, f, kappa, w, om)

time: 45.7 us -> 45 us (0.985)
  Pallas kernels: 44.9 us -> 44.3 us
where the time goes in v8:
time: 45 us; the launch traced here: 44.9 us
  Pallas kernels  44.3 us (98%)
  between operations  0.64 us (1%)
    pallas_call x1, Pallas kernels, local(): pl.pallas_call(kernel, out_shape=(pltpu.VMEM((4, 2, ROWS, LANES), F32), p...  43.3 us
    pallas_call x1, Pallas kernels, local(): pl.pallas_call(unpack_kernel, out_shape=(jax.ShapeDtypeStruct((ROWS * ROW...  0.97 us

profile of v8, /device:TPU:0, one launch (start us, length us, event | category | flops | bytes accessed | tf_op | source)
XLA Modules:
  0.0 44.9 jit_solution(15504942949405601908)
XLA Ops:
  0.6 43.3 %shard_map.68 = (f32[4,2,32,128]{3,2,1,0:T(8,128)S(1)}, f32[8,128]{1,0:T(8,128)S(1)}) custom-call(f32[32,32,32]{2,1,0:T(8,128)} %u_ref.1, f32[32,32,32]{2,1,0:T(8,128)} %f_ref.1, f32[32,32,32]{2,1,0:T(8,128)} %k_ref.1, f32[26]{0:T(128)} %w_hbm.1, f32[32]{0:T(128)} %om_hbm.1), custom_call_target="tpu_custom_call" | custom-call | tf_op jit(solution)/shard_map/pallas_call | solution.py:391
  43.9 1.0 %shard_map.69 = (f32[1024,32]{1,0:T(8,128)}, f32[1,32]{1,0:T(1,128)}) custom-call(f32[4,2,32,128]{3,2,1,0:T(8,128)S(1)} %get-tuple-element.6.dense_ref, f32[8,128]{1,0:T(8,128)S(1)} %get-tuple-element.7.total_ref), custom_call_target="tpu_custom_call" | custom-call | tf_op jit(solution)/shard_map/pallas_call | solution.py:420

commit v9 on v8

--- a/solution.py
+++ b/solution.py
@@ -158,32 +158,6 @@
     send_own(1)
     pack_array(2)
     send_own(2)
-
-    wait_own(0)
-    unpack_own(0, lambda v: put(kap, 8, v))
-    kap_copy(fast, 0).start()
-    for part in range(2):
-        kap_copy(slow, part).start()
-    wait_own(1)
-
-    def store_u(v):
-        stage[:, 0:ROWS, :] = v
-        put(fld, 8, v)
-    unpack_own(1, store_u)
-    u_copy(2, fast, 0).start()
-    for part in range(2):
-        u_copy(2, slow, part).start()
-    kap_copy(fast, 1).start()
-    wait_own(2)
-
-    def store_f(v):
-        src_own[8:16] = v
-    unpack_own(2, store_f)
-    f_copy(fast, 0).start()
-    for part in range(2):
-        f_copy(slow, part).start()
-    u_copy(2, fast, 1).start()
-    f_copy(fast, 1).start()
 
     loads[3].wait()
     loads[4].wait()
@@ -217,13 +191,39 @@
     def scale_range(lo, hi):
         lax.fori_loop(lo, hi, scale_f, 0)
 
-    sums[...] = jnp.zeros_like(sums)
+    wait_own(0)
+    unpack_own(0, lambda v: put(kap, 8, v))
+    kap_copy(fast, 0).start()
+    for part in range(2):
+        kap_copy(slow, part).start()
     coef_range(9, 15)
-    scale_range(9, 15)
+    wait_own(1)
+
+    def store_u(v):
+        stage[:, 0:ROWS, :] = v
+        put(fld, 8, v)
+    unpack_own(1, store_u)
+    u_copy(2, fast, 0).start()
+    for part in range(2):
+        u_copy(2, slow, part).start()
+    kap_copy(fast, 1).start()
     for part in range(2):
         kap_copy(fast, part).wait_recv()
         unpack_side(0, kap, fast, part)
     coef_range(1 + 14 * fast, 9 + 14 * fast)
+    wait_own(2)
+
+    def store_f(v):
+        src_own[8:16] = v
+    unpack_own(2, store_f)
+    f_copy(fast, 0).start()
+    for part in range(2):
+        f_copy(slow, part).start()
+    u_copy(2, fast, 1).start()
+    f_copy(fast, 1).start()
+
+    sums[...] = jnp.zeros_like(sums)
+    scale_range(9, 15)
 
     def slow_setup(part, left):
         lo = left + slow * (20 - 2 * left)

time: 45 us -> 44.8 us (level)
  no operation moved by 1% of the time
where the time goes in v9:
time: 44.8 us; the launch traced here: 44.6 us
  Pallas kernels  44 us (98%)
  between operations  0.64 us (1%)
    pallas_call x1, Pallas kernels, local(): pl.pallas_call(kernel, out_shape=(pltpu.VMEM((4, 2, ROWS, LANES), F32), p...  43 us
    pallas_call x1, Pallas kernels, local(): pl.pallas_call(unpack_kernel, out_shape=(jax.ShapeDtypeStruct((ROWS * ROW...  0.97 us

profile of v9, /device:TPU:0, one launch (start us, length us, event | category | flops | bytes accessed | tf_op | source)
XLA Modules:
  0.0 44.6 jit_solution(1832289797382411644)
XLA Ops:
  0.6 43.0 %shard_map.68 = (f32[4,2,32,128]{3,2,1,0:T(8,128)S(1)}, f32[8,128]{1,0:T(8,128)S(1)}) custom-call(f32[32,32,32]{2,1,0:T(8,128)} %u_ref.1, f32[32,32,32]{2,1,0:T(8,128)} %f_ref.1, f32[32,32,32]{2,1,0:T(8,128)} %k_ref.1, f32[26]{0:T(128)} %w_hbm.1, f32[32]{0:T(128)} %om_hbm.1), custom_call_target="tpu_custom_call" | custom-call | tf_op jit(solution)/shard_map/pallas_call | solution.py:391
  43.7 1.0 %shard_map.69 = (f32[1024,32]{1,0:T(8,128)}, f32[1,32]{1,0:T(1,128)}) custom-call(f32[4,2,32,128]{3,2,1,0:T(8,128)S(1)} %get-tuple-element.6.dense_ref, f32[8,128]{1,0:T(8,128)S(1)} %get-tuple-element.7.total_ref), custom_call_target="tpu_custom_call" | custom-call | tf_op jit(solution)/shard_map/pallas_call | solution.py:420

commit v10 on v9

--- a/solution.py
+++ b/solution.py
@@ -273,7 +273,7 @@
         before = strip(1, 9, 3, 0, 8, blk)
         before = flush(strip(1, 9, 3, 1, before, blk))
         before = flush(strip(2, 10, 4, 0, before, blk))
-        before = flush(strip(3, 11, 2, 0, before, blk))
+        before = strip(3, 11, 2, 0, before, blk)
 
         @pl.when(blk == 0)
         def _():

time: 44.8 us -> 44.8 us (level)
  no operation moved by 1% of the time
where the time goes in v10:
time: 44.8 us; the launch traced here: 44.6 us
  Pallas kernels  44 us (98%)
  between operations  0.64 us (1%)
    pallas_call x1, Pallas kernels, local(): pl.pallas_call(kernel, out_shape=(pltpu.VMEM((4, 2, ROWS, LANES), F32), p...  43 us
    pallas_call x1, Pallas kernels, local(): pl.pallas_call(unpack_kernel, out_shape=(jax.ShapeDtypeStruct((ROWS * ROW...  0.97 us

profile of v10, /device:TPU:0, one launch (start us, length us, event | category | flops | bytes accessed | tf_op | source)
XLA Modules:
  0.0 44.6 jit_solution(13978976302951655424)
XLA Ops:
  0.6 43.0 %shard_map.68 = (f32[4,2,32,128]{3,2,1,0:T(8,128)S(1)}, f32[8,128]{1,0:T(8,128)S(1)}) custom-call(f32[32,32,32]{2,1,0:T(8,128)} %u_ref.1, f32[32,32,32]{2,1,0:T(8,128)} %f_ref.1, f32[32,32,32]{2,1,0:T(8,128)} %k_ref.1, f32[26]{0:T(128)} %w_hbm.1, f32[32]{0:T(128)} %om_hbm.1), custom_call_target="tpu_custom_call" | custom-call | tf_op jit(solution)/shard_map/pallas_call | solution.py:391
  43.7 1.0 %shard_map.69 = (f32[1024,32]{1,0:T(8,128)}, f32[1,32]{1,0:T(1,128)}) custom-call(f32[4,2,32,128]{3,2,1,0:T(8,128)S(1)} %get-tuple-element.6.dense_ref, f32[8,128]{1,0:T(8,128)S(1)} %get-tuple-element.7.total_ref), custom_call_target="tpu_custom_call" | custom-call | tf_op jit(solution)/shard_map/pallas_call | solution.py:420

commit v11 on v10

--- a/solution.py
+++ b/solution.py
@@ -337,6 +337,14 @@
             send_sem=back_send.at[yy, r - 1], recv_sem=back_recv_sem.at[yy, r - 1],
             device_id=partner(r), device_id_type=MESH)
 
+    flat = jnp.sum(sums[...], axis=1)
+    flat = jnp.concatenate([flat, jnp.zeros((96, LANES), F32)], axis=0)
+    mine = jnp.sum(flat.T, axis=0, keepdims=True)
+    mine = jnp.broadcast_to(mine, (8, LANES))
+    psum[8] = mine
+    psum[me] = mine
+    for r in range(1, 8):
+        sum_copy(r).start()
     flat_stage = stage.reshape(8 * PITCH, LANES)
     for yy in range(2):
         tiles = [flat_stage[pl.ds(16 * yy + x, 8, stride=PITCH), :] for x in range(16)]
@@ -347,14 +355,6 @@
         for r in range(1, 4):
             back_copy(r, yy).start()
     back_recv[my_l] = back[my_q]
-    flat = jnp.sum(sums[...], axis=1)
-    flat = jnp.concatenate([flat, jnp.zeros((96, LANES), F32)], axis=0)
-    mine = jnp.sum(flat.T, axis=0, keepdims=True)
-    mine = jnp.broadcast_to(mine, (8, LANES))
-    psum[8] = mine
-    psum[me] = mine
-    for r in range(1, 8):
-        sum_copy(r).start()
 
     for r in range(1, 4):
         for yy in range(2):

time: 44.8 us -> 44.7 us (level)
  no operation moved by 1% of the time
where the time goes in v11:
time: 44.7 us; the launch traced here: 44.6 us
  Pallas kernels  43.9 us (98%)
  between operations  0.64 us (1%)
    pallas_call x1, Pallas kernels, local(): pl.pallas_call(kernel, out_shape=(pltpu.VMEM((4, 2, ROWS, LANES), F32), p...  43 us
    pallas_call x1, Pallas kernels, local(): pl.pallas_call(unpack_kernel, out_shape=(jax.ShapeDtypeStruct((ROWS * ROW...  0.97 us

profile of v11, /device:TPU:0, one launch (start us, length us, event | category | flops | bytes accessed | tf_op | source)
XLA Modules:
  0.0 44.6 jit_solution(14510051059284418507)
XLA Ops:
  0.6 43.0 %shard_map.68 = (f32[4,2,32,128]{3,2,1,0:T(8,128)S(1)}, f32[8,128]{1,0:T(8,128)S(1)}) custom-call(f32[32,32,32]{2,1,0:T(8,128)} %u_ref.1, f32[32,32,32]{2,1,0:T(8,128)} %f_ref.1, f32[32,32,32]{2,1,0:T(8,128)} %k_ref.1, f32[26]{0:T(128)} %w_hbm.1, f32[32]{0:T(128)} %om_hbm.1), custom_call_target="tpu_custom_call" | custom-call | tf_op jit(solution)/shard_map/pallas_call | solution.py:391
  43.6 1.0 %shard_map.69 = (f32[1024,32]{1,0:T(8,128)}, f32[1,32]{1,0:T(1,128)}) custom-call(f32[4,2,32,128]{3,2,1,0:T(8,128)S(1)} %get-tuple-element.6.dense_ref, f32[8,128]{1,0:T(8,128)S(1)} %get-tuple-element.7.total_ref), custom_call_target="tpu_custom_call" | custom-call | tf_op jit(solution)/shard_map/pallas_call | solution.py:420
